TPU v7x, 512 devices: a whole 4x8x8 slice. The times are simulated.
512 devices in a mesh: cp: 128 (over z, y, core), tp: 4 (over x).
Axes of the slice: x: 4, y: 8, z: 8, core: 2. Of those that a mesh axis runs over, the one named last changes fastest.
Arguments:
- queries: bfloat16 [49152, 4096], P('cp', 'tp'), may hold values from -56 to 56
- keys: bfloat16 [49152, 1024], P('cp', 'tp'), may hold values from -6 to 6
- values: bfloat16 [49152, 1024], P('cp', 'tp'), may hold values from -6 to 6
- lengths: int32 [32], replicated, may hold values from 1 to 2689, 49152 in all
Outputs:
- attended: bfloat16 [49152, 4096], P('cp', 'tp')
Inputs may be any that keep to these rules, and one draw needn't show every extreme that they name: `lengths`: the 32 documents fill the 49152 tokens; each has at most 2689 tokens and one has exactly 2689.
All inputs are finite; a program needn't handle non-finite values.
Results may differ from a plain program's by a relative error of at most 0.0065.
Values may be sent and summed in bfloat16 or wider, within the bound.
A program may use at most 64 MiB of HBM per device.

v0:
```python
import jax
import jax.numpy as jnp
from jax import lax
from jax.sharding import PartitionSpec as P

HEAD_DIM = 128
LEVELS = 3


def passed_along(value, axis, steps):
    count = lax.axis_size(axis)
    leading, last = (max(0, -steps), min(count, count - steps))
    return lax.ppermute(value, axis, [(source, source + steps) for source in range(leading, last)])


def document_of(doc_starts, position):
    return jnp.sum((doc_starts[None, :] <= position[:, None]).astype(jnp.int32), axis=1) - 1


def body(queries, keys, values, lengths):
    tok_rows = queries.shape[0]
    kv_heads = keys.shape[1] // HEAD_DIM
    group_size = queries.shape[1] // keys.shape[1]
    logit_scale_factor = HEAD_DIM ** (-0.5)
    doc_ends = jnp.cumsum(lengths)
    doc_starts = doc_ends - lengths
    anchor = lax.axis_index("cp") * tok_rows
    reach_blocks = min(2**LEVELS, lax.axis_size("cp"))
    query_pos = anchor + jnp.arange(tok_rows, dtype=jnp.int32)
    query_doc = document_of(doc_starts, query_pos)
    grouped = queries.reshape(tok_rows, kv_heads, group_size, HEAD_DIM).transpose(1, 2, 0, 3)
    keys_major = keys.reshape(tok_rows, kv_heads, HEAD_DIM).transpose(1, 0, 2)
    values_major = values.reshape(tok_rows, kv_heads, HEAD_DIM).transpose(1, 0, 2)
    running = (
        jnp.full((kv_heads, group_size, tok_rows), -1e30, jnp.float32),
        jnp.zeros((kv_heads, group_size, tok_rows), jnp.float32),
        jnp.zeros((kv_heads, group_size, tok_rows, HEAD_DIM), jnp.float32),
    )

    def absorb(running, key_block, value_block, key_start):
        key_pos = key_start + jnp.arange(key_block.shape[1], dtype=jnp.int32)
        allowed = query_doc[:, None] == document_of(doc_starts, key_pos)[None, :]
        allowed = allowed & (key_pos[None, :] <= query_pos[:, None]) & (key_pos[None, :] >= 0)
        max_old, denominator, weighted_value_sum = running
        attention_logits = (
            jnp.einsum("xayu,xku->xayk", grouped, key_block, preferred_element_type=jnp.float32)
            * logit_scale_factor
        )
        attention_logits = jnp.where(allowed, attention_logits, -1e30)
        max_new = jnp.maximum(max_old, jnp.max(attention_logits, axis=-1))
        weights = jnp.where(allowed, jnp.exp(attention_logits - max_new[..., None]), 0.0)
        rescale = jnp.exp(max_old - max_new)
        denominator = denominator * rescale + jnp.sum(weights, axis=-1)
        weighted_value_sum = weighted_value_sum * rescale[..., None] + jnp.einsum(
            "xayk,xkf->xayf",
            weights.astype(jnp.bfloat16),
            value_block,
            preferred_element_type=jnp.float32,
        )
        return (max_new, denominator, weighted_value_sum)

    running = absorb(running, keys_major, values_major, anchor)
    window_keys, window_values = (keys_major, values_major)
    blocks_held = 1
    while blocks_held < reach_blocks:
        got_keys, got_values = passed_along((window_keys, window_values), "cp", blocks_held)
        for segment in range(blocks_held):
            running = absorb(
                running,
                got_keys[:, segment * tok_rows : (segment + 1) * tok_rows],
                got_values[:, segment * tok_rows : (segment + 1) * tok_rows],
                anchor - (2 * blocks_held - 1 - segment) * tok_rows,
            )
        window_keys = jnp.concatenate([got_keys, window_keys], axis=1)
        window_values = jnp.concatenate([got_values, window_values], axis=1)
        blocks_held = blocks_held * 2
    max_last, denominator, weighted_value_sum = running
    result = weighted_value_sum / denominator[..., None]
    return result.transpose(2, 0, 1, 3).reshape(tok_rows, -1).astype(jnp.bfloat16)


def solution(mesh):
    in_specs = (P("cp", "tp"), P("cp", "tp"), P("cp", "tp"), P())
    out_specs = P("cp", "tp")
    return jax.shard_map(body, mesh=mesh, in_specs=in_specs, out_specs=out_specs, check_vma=False)
```

profile of v0, /device:TPU:398, one launch (start us, length us, event | category | flops | bytes accessed | tf_op | source)
XLA Modules:
  0.0 120.1 jit_solution(1341993625354651391)
XLA Ops:
  0.0 1.1 copy.33
  1.3 1.9 %collective-permute-start = (bf16[2,384,128]{2,1,0:T(8,128)(2,1)S(1)}, bf16[2,384,128]{2,1,0:T(8,128)(2,1)S(1)}, u32[]{:S(2)}, u32[]{:S(2)}) collective-permute-start(bf16[2,384,128]{2,1,0:T(8,128)(2,1)S(1)} %bitcast.370), channel_id=1, source_target_pairs={{0,4},{4,8},{8,12},{12,16},{16,20},{20,24},{24,28},{28,32},{32,36}... | collective-permute-start | bytes 589832 | tf_op jit(solution)/shard_map/ppermute | solution.py:13
  3.2 1.1 copy.35
  4.3 3.6 %collective-permute-start.1 = (bf16[2,384,128]{1,2,0:T(8,128)(2,1)S(1)}, bf16[2,384,128]{1,2,0:T(8,128)(2,1)S(1)}, u32[]{:S(2)}, u32[]{:S(2)}) collective-permute-start(bf16[2,384,128]{1,2,0:T(8,128)(2,1)S(1)} %bitcast.373), channel_id=1, source_target_pairs={{0,4},{4,8},{8,12},{12,16},{16,20},{20,24},{24,28},{28,32},{32,36}... | collective-permute-start | bytes 589832 | tf_op jit(solution)/shard_map/ppermute | solution.py:13
  9.6 1.9 %reshape.379 = bf16[384,2,4,128]{3,2,1,0:T(4,128)(2,1)S(1)} reshape(bf16[384,1024]{1,0:T(8,128)(2,1)} %param.4) | data formatting | bytes 1572864 | tf_op jit(solution)/shard_map/reshape | solution.py:31
  11.8 1.3 %and_and_fusion.7 = (pred[384,384]{0,1:T(8,128)(4,1)S(1)}, pred[384,384]{0,1:T(8,128)(4,1)S(1)}, pred[384,384]{0,1:T(8,128)(4,1)S(1)}, pred[384,384]{0,1:T(8,128...) fusion(s32[384]{0:T(512)S(1)} %iota_add_fusion.7, s32[384]{0:T(512)S(1)} %get-tuple-element.63, ...), kind=kLoop, calls=%fused_computation.98 | loop fusion | flops 3538944 | bytes 905472 | tf_op jit(solution)/shard_map/and | solution.py:43
  14.7 3.5 %collective-permute-start.2 = (bf16[2,768,128]{2,1,0:T(8,128)(2,1)S(1)}, bf16[2,768,128]{2,1,0:T(8,128)(2,1)S(1)}, u32[]{:S(2)}, u32[]{:S(2)}) collective-permute-start(bf16[2,768,128]{2,1,0:T(8,128)(2,1)S(1)} %pad_maximum_fusion.2), channel_id=1, source_target_pairs={{0,8},{4,12},{8,16},{12,20},{16,24},{20,28},{24,32},{28,36},{32,40... | collective-permute-start | bytes 1179656 | tf_op jit(solution)/shard_map/ppermute | solution.py:13
  18.2 4.7 %collective-permute-start.3 = (bf16[2,768,128]{1,2,0:T(8,128)(2,1)S(1)}, bf16[2,768,128]{1,2,0:T(8,128)(2,1)S(1)}, u32[]{:S(2)}, u32[]{:S(2)}) collective-permute-start(bf16[2,768,128]{1,2,0:T(8,128)(2,1)S(1)} %pad_maximum_fusion.3), channel_id=1, source_target_pairs={{0,8},{4,12},{8,16},{12,20},{16,24},{20,28},{24,32},{28,36},{32,40... | collective-permute-start | bytes 1179656 | tf_op jit(solution)/shard_map/ppermute | solution.py:13
  23.9 4.7 %collective-permute-done.2 = bf16[2,768,128]{2,1,0:T(8,128)(2,1)S(1)} collective-permute-done((bf16[2,768,128]{2,1,0:T(8,128)(2,1)S(1)}, bf16[2,768,128]{2,1,0:T(8,128)(2,1)S(1)}, u32[]{:S(2)}, u32[]{:S(2)}) %collective-permute-start.2) | collective-permute-done | bytes 393248 | tf_op jit(solution)/shard_map/ppermute | solution.py:13
  28.6 5.7 %collective-permute-start.4 = (bf16[2,1536,128]{2,1,0:T(8,128)(2,1)S(1)}, bf16[2,1536,128]{2,1,0:T(8,128)(2,1)S(1)}, u32[]{:S(2)}, u32[]{:S(2)}) collective-permute-start(bf16[2,1536,128]{2,1,0:T(8,128)(2,1)S(1)} %pad_maximum_fusion), channel_id=1, source_target_pairs={{0,16},{4,20},{8,24},{12,28},{16,32},{20,36},{24,40},{28,44},{32,4... | collective-permute-start | bytes 2359304 | tf_op jit(solution)/shard_map/ppermute | solution.py:13
  34.4 4.3 %collective-permute-done.3 = bf16[2,768,128]{1,2,0:T(8,128)(2,1)S(1)} collective-permute-done((bf16[2,768,128]{1,2,0:T(8,128)(2,1)S(1)}, bf16[2,768,128]{1,2,0:T(8,128)(2,1)S(1)}, u32[]{:S(2)}, u32[]{:S(2)}) %collective-permute-start.3) | collective-permute-done | bytes 393248 | tf_op jit(solution)/shard_map/ppermute | solution.py:13
  38.7 5.0 %collective-permute-start.5 = (bf16[2,1536,128]{1,2,0:T(8,128)(2,1)S(1)}, bf16[2,1536,128]{1,2,0:T(8,128)(2,1)S(1)}, u32[]{:S(2)}, u32[]{:S(2)}) collective-permute-start(bf16[2,1536,128]{1,2,0:T(8,128)(2,1)S(1)} %pad_maximum_fusion.1), channel_id=1, source_target_pairs={{0,16},{4,20},{8,24},{12,28},{16,32},{20,36},{24,40},{28,44},{32,4... | collective-permute-start | bytes 2359304 | tf_op jit(solution)/shard_map/ppermute | solution.py:13
  44.7 3.1 %fusion.2 = (f32[2,4,384]{2,1,0:T(4,128)S(1)}, f32[2,384,4,384]{3,1,2,0:T(8,128)}) fusion(pred[384,384]{0,1:T(8,128)(4,1)S(1)} %get-tuple-element.39, bf16[384,2,4,128]{3,2,1,0:T(4,128)(2,1)S(1)} %reshape.379, bf16[2,768,128]{2,1,0:T(8,128)(2,1)S(1)} %collective-permute-done.2), kind=kOutput, calls=%fused_computation.18 | convolution fusion | flops 305525760 | bytes 5861376 | tf_op jit(solution)/shard_map/xayu,xku->xayk/dot_general | solution.py:46
  47.7 41.8 %collective-permute-done.4 = bf16[2,1536,128]{2,1,0:T(8,128)(2,1)S(1)} collective-permute-done((bf16[2,1536,128]{2,1,0:T(8,128)(2,1)S(1)}, bf16[2,1536,128]{2,1,0:T(8,128)(2,1)S(1)}, u32[]{:S(2)}, u32[]{:S(2)}) %collective-permute-start.4) | collective-permute-done | bytes 786464 | tf_op jit(solution)/shard_map/ppermute | solution.py:13
  89.6 1.0 fusion.7
  93.5 1.2 fusion.8
  94.6 2.7 %fusion.38 = f32[2,4,384,128]{2,3,1,0:T(8,128)} fusion(bf16[2,384,128,1]{1,2,3,0:T(8,128)(2,1)S(1)} %bitcast.376, f32[2,4,384,384]{2,3,1,0:T(8,128)S(1)} %get-tuple-element.55, f32[2,4,384]{2,1,0:T(4,128)S(1)} %get-tuple-element.31, pred[384,384]{0,1:T(8,128)(4,1)S(1)} %get-tuple-element.32), kind=kOutput, calls=%fused_computation.47 | convolution fusion | flops 307888128 | bytes 6647808 | tf_op jit(solution)/shard_map/xayk,xkf->xayf/dot_general | solution.py:54
  97.3 1.2 fusion.16
  98.5 1.2 fusion.18
  99.6 1.1 fusion.22
  100.8 1.4 %fusion.20 = f32[2,4,384]{2,1,0:T(4,128)S(1)} fusion(f32[2,384,4,384]{3,1,2,0:T(8,128)S(1)} %get-tuple-element.43, f32[2,4,384]{2,1,0:T(4,128)S(1)} %get-tuple-element.23, pred[384,384]{0,1:T(8,128)(4,1)S(1)} %get-tuple-element.36), kind=kLoop, calls=%fused_computation.36 | loop fusion | flops 5895168 | bytes 4890624 | tf_op jit(solution)/shard_map/reduce_sum | solution.py:53
  102.2 1.2 fusion.14
  103.4 1.2 fusion.12
  104.5 1.2 fusion.10
  105.7 2.7 %fusion.34 = f32[2,4,384,128]{2,3,1,0:T(8,128)} fusion(f32[2,384,4,384]{3,1,2,0:T(8,128)S(1)} %bitcast.369, f32[2,4,384]{2,1,0:T(4,128)S(1)} %get-tuple-element.27, pred[384,384]{0,1:T(8,128)(4,1)S(1)} %get-tuple-element.39, bf16[2,768,128]{1,2,0:T(8,128)(2,1)S(1)} %collective-permute-done.3), kind=kOutput, calls=%fused_computation.45 | convolution fusion | flops 307888128 | bytes 6647808 | tf_op jit(solution)/shard_map/xayk,xkf->xayf/dot_general | solution.py:54
  108.4 1.5 %fusion.36 = f32[2,4,384,128]{2,3,1,0:T(8,128)S(1)} fusion(f32[2,4,384,384]{2,3,1,0:T(8,128)S(1)} %get-tuple-element.53, f32[2,4,384]{2,1,0:T(4,128)S(1)} %get-tuple-element.28, pred[384,384]{0,1:T(8,128)(4,1)S(1)} %get-tuple-element.38, bf16[2,384,128]{1,2,0:T(8,128)(2,1)S(1)} %collective-permute-done.1), kind=kOutput, calls=%fused_computation.46 | convolution fusion | flops 307888128 | bytes 6647808 | tf_op jit(solution)/shard_map/xayk,xkf->xayf/dot_general | solution.py:54
  110.0 1.5 %fusion.32 = f32[2,4,384,128]{2,3,1,0:T(8,128)S(1)} fusion(f32[2,384,4,384]{3,1,2,0:T(8,128)S(1)} %get-tuple-element.49, f32[2,4,384]{2,1,0:T(4,128)S(1)} %get-tuple-element.26, pred[384,384]{0,1:T(8,128)(4,1)S(1)} %get-tuple-element.33, bf16[2,768,128]{1,2,0:T(8,128)(2,1)S(1)} %collective-permute-done.3), kind=kOutput, calls=%fused_computation.44 | convolution fusion | flops 307888128 | bytes 6647808 | tf_op jit(solution)/shard_map/xayk,xkf->xayf/dot_general | solution.py:54
  111.6 1.5 %fusion.30 = f32[2,4,384,128]{2,3,1,0:T(8,128)S(1)} fusion(f32[2,384,4,384]{3,1,2,0:T(8,128)S(1)} %get-tuple-element.47, f32[2,4,384]{2,1,0:T(4,128)S(1)} %get-tuple-element.25, pred[384,384]{0,1:T(8,128)(4,1)S(1)} %get-tuple-element.34, bf16[2,1536,128]{1,2,0:T(8,128)(2,1)S(1)} %collective-permute-done.5), kind=kOutput, calls=%fused_computation.43 | convolution fusion | flops 307888128 | bytes 6647808 | tf_op jit(solution)/shard_map/xayk,xkf->xayf/dot_general | solution.py:54
  113.1 1.5 %fusion.28 = f32[2,4,384,128]{2,3,1,0:T(8,128)S(1)} fusion(f32[2,384,4,384]{3,1,2,0:T(8,128)S(1)} %get-tuple-element.45, f32[2,4,384]{2,1,0:T(4,128)S(1)} %get-tuple-element.24, pred[384,384]{0,1:T(8,128)(4,1)S(1)} %get-tuple-element.35, bf16[2,1536,128]{1,2,0:T(8,128)(2,1)S(1)} %collective-permute-done.5), kind=kOutput, calls=%fused_computation.42 | convolution fusion | flops 307888128 | bytes 6647808 | tf_op jit(solution)/shard_map/xayk,xkf->xayf/dot_general | solution.py:54
  114.6 1.5 %fusion.26 = f32[2,4,384,128]{2,3,1,0:T(8,128)S(1)} fusion(f32[2,384,4,384]{3,1,2,0:T(8,128)S(1)} %get-tuple-element.43, f32[2,4,384]{2,1,0:T(4,128)S(1)} %get-tuple-element.23, pred[384,384]{0,1:T(8,128)(4,1)S(1)} %get-tuple-element.36, bf16[2,1536,128]{1,2,0:T(8,128)(2,1)S(1)} %collective-permute-done.5), kind=kOutput, calls=%fused_computation.41 | convolution fusion | flops 307888128 | bytes 6647808 | tf_op jit(solution)/shard_map/xayk,xkf->xayf/dot_general | solution.py:54
  116.5 2.4 %fusion.49 = bf16[384,2,4,128]{0,3,2,1:T(8,128)(2,1)S(1)} fusion(f32[2,4,384,128]{2,3,1,0:T(8,128)S(1)} %fusion.26, f32[2,4,384,128]{2,3,1,0:T(8,128)S(1)} %fusion.28, f32[2,4,384,128]{2,3,1,0:T(8,128)S(1)} %fusion.30, f32[2,4,384,128]{2,3,1,0:T(8,128)S(1)} %fusion.32, f32[2,4,384,128]{2,3,1,0:T(8,128)S(1)} %copy-done.1, ...), kind=kOutput, calls=%fused_computation.58 | convolution fusion | flops 314572800 | bytes 16982016 | tf_op jit(solution)/shard_map/xayk,xkf->xayf/dot_general | solution.py:54
  118.9 1.2 copy.44
  (48 shorter events, 8.9 us)
Async XLA Ops:
  1.3 13.4 %collective-permute-start = (bf16[2,384,128]{2,1,0:T(8,128)(2,1)S(1)}, bf16[2,384,128]{2,1,0:T(8,128)(2,1)S(1)}, u32[]{:S(2)}, u32[]{:S(2)}) collective-permute-start(bf16[2,384,128]{2,1,0:T(8,128)(2,1)S(1)} %bitcast.370), channel_id=1, source_target_pairs={{0,4},{4,8},{8,12},{12,16},{16,20},{20,24},{24,28},{28,32},{32,36}... | collective-permute-start | bytes 589832 | tf_op jit(solution)/shard_map/ppermute | solution.py:13
  4.3 13.9 %collective-permute-start.1 = (bf16[2,384,128]{1,2,0:T(8,128)(2,1)S(1)}, bf16[2,384,128]{1,2,0:T(8,128)(2,1)S(1)}, u32[]{:S(2)}, u32[]{:S(2)}) collective-permute-start(bf16[2,384,128]{1,2,0:T(8,128)(2,1)S(1)} %bitcast.373), channel_id=1, source_target_pairs={{0,4},{4,8},{8,12},{12,16},{16,20},{20,24},{24,28},{28,32},{32,36}... | collective-permute-start | bytes 589832 | tf_op jit(solution)/shard_map/ppermute | solution.py:13
  14.7 13.9 %collective-permute-start.2 = (bf16[2,768,128]{2,1,0:T(8,128)(2,1)S(1)}, bf16[2,768,128]{2,1,0:T(8,128)(2,1)S(1)}, u32[]{:S(2)}, u32[]{:S(2)}) collective-permute-start(bf16[2,768,128]{2,1,0:T(8,128)(2,1)S(1)} %pad_maximum_fusion.2), channel_id=1, source_target_pairs={{0,8},{4,12},{8,16},{12,20},{16,24},{20,28},{24,32},{28,36},{32,40... | collective-permute-start | bytes 1179656 | tf_op jit(solution)/shard_map/ppermute | solution.py:13
  18.2 20.4 %collective-permute-start.3 = (bf16[2,768,128]{1,2,0:T(8,128)(2,1)S(1)}, bf16[2,768,128]{1,2,0:T(8,128)(2,1)S(1)}, u32[]{:S(2)}, u32[]{:S(2)}) collective-permute-start(bf16[2,768,128]{1,2,0:T(8,128)(2,1)S(1)} %pad_maximum_fusion.3), channel_id=1, source_target_pairs={{0,8},{4,12},{8,16},{12,20},{16,24},{20,28},{24,32},{28,36},{32,40... | collective-permute-start | bytes 1179656 | tf_op jit(solution)/shard_map/ppermute | solution.py:13
  28.6 60.9 %collective-permute-start.4 = (bf16[2,1536,128]{2,1,0:T(8,128)(2,1)S(1)}, bf16[2,1536,128]{2,1,0:T(8,128)(2,1)S(1)}, u32[]{:S(2)}, u32[]{:S(2)}) collective-permute-start(bf16[2,1536,128]{2,1,0:T(8,128)(2,1)S(1)} %pad_maximum_fusion), channel_id=1, source_target_pairs={{0,16},{4,20},{8,24},{12,28},{16,32},{20,36},{24,40},{28,44},{32,4... | collective-permute-start | bytes 2359304 | tf_op jit(solution)/shard_map/ppermute | solution.py:13
  38.7 72.8 %collective-permute-start.5 = (bf16[2,1536,128]{1,2,0:T(8,128)(2,1)S(1)}, bf16[2,1536,128]{1,2,0:T(8,128)(2,1)S(1)}, u32[]{:S(2)}, u32[]{:S(2)}) collective-permute-start(bf16[2,1536,128]{1,2,0:T(8,128)(2,1)S(1)} %pad_maximum_fusion.1), channel_id=1, source_target_pairs={{0,16},{4,20},{8,24},{12,28},{16,32},{20,36},{24,40},{28,44},{32,4... | collective-permute-start | bytes 2359304 | tf_op jit(solution)/shard_map/ppermute | solution.py:13
  99.6 3.7 %slice-start = ((s8[4718592]{0:T(1024)(128)(4,1)}), s8[4194304]{0:T(1024)(128)(4,1)S(1)}, s32[]{:S(2)}) async-start(s8[4718592]{0:T(1024)(128)(4,1)} %bitcast.368), calls=%async_computation | async-start | bytes 8388608
  100.8 2.6 %slice-start.1 = ((s8[4718592]{0:T(1024)(128)(4,1)}), s8[524288]{0:T(1024)(128)(4,1)S(1)}, s32[]{:S(2)}) async-start(s8[4718592]{0:T(1024)(128)(4,1)} %bitcast.368), calls=%async_computation.1 | async-start | bytes 1048576
  114.6 1.6 %copy-start = (f32[2,4,384,128]{2,3,1,0:T(8,128)S(1)}, f32[2,4,384,128]{2,3,1,0:T(8,128)}, u32[]{:S(2)}) copy-start(f32[2,4,384,128]{2,3,1,0:T(8,128)} %fusion.38) | copy-start | bytes 4718596
  114.6 1.9 %copy-start.1 = (f32[2,4,384,128]{2,3,1,0:T(8,128)S(1)}, f32[2,4,384,128]{2,3,1,0:T(8,128)}, u32[]{:S(2)}) copy-start(f32[2,4,384,128]{2,3,1,0:T(8,128)} %fusion.34) | copy-start | bytes 4718596
where the time goes:
time: 120 us
  waiting for transfers between devices  50.8 us (42%)
  matrix products  25.3 us (21%)
  starting transfers between devices  24.4 us (20%)
  other arithmetic  12.7 us (11%)
  local copies, waits for them, and re-layouts  6.54 us (5%)
    ppermute x6, waiting for transfers between devices, passed_along(): lax.ppermute(value, axis, [(source, source + steps) for source in range(l...  50.8 us
    ppermute x6, starting transfers between devices, passed_along(): lax.ppermute(value, axis, [(source, source + steps) for source in range(l...  24.4 us
    dot_general x8, matrix products, absorb(): jnp.einsum('xayk,xkf->xayf', weights.astype(jnp.bfloat16), value_block, p...  15.4 us
    dot_general x8, matrix products, absorb(): jnp.einsum('xayu,xku->xayk', grouped, key_block, preferred_element_type=j...  9.82 us
    reduce_sum x8, other arithmetic, absorb(): denominator = denominator * rescale + jnp.sum(weights, axis=-1)  9.46 us
    unnamed x10, local copies, waits for them, and re-layouts  2.52 us
  transfers between devices with their start and end apart: 6, of which 3 were waited for; matrix products, arithmetic and copies ran while one was open for 29% of the time, Pallas kernels for 0%

commit v1 on v0

v1 whole, which is shorter than its diff:
```python
import functools
import math

import jax
import jax.numpy as jnp
from jax import lax
from jax.experimental import pallas as pl
from jax.experimental.pallas import tpu as pltpu
from jax.sharding import PartitionSpec as P

HEAD_DIM = 128
RING_Y = 8
HALVES = ((0, 256), (256, 128))
MASKED = -1e30
FAR = 6
LANDED = 7
RELAY = 8
OWN = 9
SLOTS = 10


def kernel(count, q_hbm, k_hbm, v_hbm, lengths, out_hbm,
           kv, q_in, qt, acc, top, total, first_live, bias, out_v,
           load_sem, out_sem, recv_sem, own_sem, relay_sem, cross_sem):
    toks = q_in.shape[0]
    heads = q_in.shape[1] // HEAD_DIM
    group = heads // (k_hbm.shape[1] // HEAD_DIM)
    factor = HEAD_DIM ** -0.5 * math.log2(math.e)
    cp = lax.axis_index("cp")
    chip, core = cp // 2, lax.rem(cp, 2)
    chips = count // 2
    y = lax.rem(chip, RING_Y)
    row = chip - y

    def core_of(which_chip):
        return lax.rem(which_chip + chips, chips) * 2 + core

    partner = chip * 2 + (1 - core)
    after, before = core_of(chip + 1), core_of(chip - 1)
    three_down = core_of(row + lax.rem(y + RING_Y - 3, RING_Y))
    three_up = core_of(row + lax.rem(y + 3, RING_Y))
    relay_to = core_of(row + lax.rem(y + 3, RING_Y) + 4)
    owner = lax.rem(chip - 4 + chips, chips)
    owner_y = lax.rem(owner, RING_Y)
    relay_from = core_of(owner - owner_y + lax.rem(owner_y + RING_Y - 3, RING_Y))

    def piece(slot, p):
        first, rows = HALVES[p // 2]
        return kv.at[p % 2, slot, pl.ds(first, rows), :]

    def remote(src, dst, send, recv, to):
        return pltpu.make_async_remote_copy(
            src_ref=src, dst_ref=dst, send_sem=send, recv_sem=recv,
            device_id={"cp": to}, device_id_type=pl.DeviceIdType.MESH)

    loads = []
    for source, target, sem in ((k_hbm, kv.at[0, OWN], 0), (v_hbm, kv.at[1, OWN], 1), (q_hbm, q_in, 2)):
        copy = pltpu.make_async_copy(source, target, load_sem.at[sem])
        copy.start()
        loads.append(copy)

    barrier = pltpu.get_barrier_semaphore()

    def greet(devices):
        for device in devices:
            pl.semaphore_signal(barrier, inc=1, device_id={"cp": device}, device_id_type=pl.DeviceIdType.MESH)
        pl.semaphore_wait(barrier, len(devices))

    @pl.when(core == 0)
    def _():
        greet((partner, after, before))

    @pl.when(core == 1)
    def _():
        greet((partner, after, before, three_down, three_up, relay_to, relay_from))

    loads[0].wait()
    loads[1].wait()

    def own_send(lane, p):
        to, slot = ((after, core), (partner, FAR), (three_down, RELAY))[lane]
        return remote(piece(OWN, p), piece(slot, p), own_sem.at[lane, p], recv_sem.at[slot, p], to)

    def relay(slot, p):
        to, target = {0: (after, 2), 1: (after, 3), 2: (after, 4), RELAY: (relay_to, LANDED), LANDED: (before, 5)}[slot]
        return remote(piece(slot, p), piece(target, p), relay_sem.at[slot, p], recv_sem.at[target, p], to)

    def cross(slot, p):
        target = FAR if slot == LANDED else slot
        return remote(piece(slot, p), piece(target, p), cross_sem.at[slot, p], recv_sem.at[target, p], partner)

    def arrived(slot, p):
        remote(piece(slot, p), piece(slot, p), cross_sem.at[slot, p], recv_sem.at[slot, p], partner).wait_recv()

    relayed = {0: (0, 2), 1: (1, RELAY, LANDED)}
    crossed = {0: (0, 2, 4), 1: (1, 3, LANDED, 5)}
    own_lanes = {0: (0, 1), 1: (0, 2)}

    def event(me, slot, pieces):
        for p in pieces:
            arrived(slot, p)
            if slot in relayed[me]:
                relay(slot, p).start()
            if slot in crossed[me]:
                cross(slot, p).start()

    def on(me, *ops):
        @pl.when(core == me)
        def _():
            for op in ops:
                event(me, *op)

    for me in (0, 1):
        @pl.when(core == me)
        def _():
            for p in range(4):
                for lane in own_lanes[me]:
                    own_send(lane, p).start()

    query_pos = cp * toks + lax.broadcasted_iota(jnp.int32, (1, toks), 1)
    starts = jnp.zeros((1, toks), jnp.int32)
    position = jnp.int32(0)
    for doc in range(lengths.shape[0]):
        starts = jnp.where(query_pos >= position, position, starts)
        position = position + lengths[doc]
    first_live[...] = starts

    loads[2].wait()
    for h in range(heads):
        qt[h] = q_in[:, h * HEAD_DIM : (h + 1) * HEAD_DIM].T
    acc[...] = jnp.zeros_like(acc)
    total[...] = jnp.zeros_like(total)
    top[...] = jnp.full_like(top, MASKED)

    def absorb(slot, half, block, diagonal=False):
        first, rows = HALVES[half]
        key_pos = block * toks + first + lax.broadcasted_iota(jnp.int32, (rows, toks), 0)
        live = key_pos >= first_live[...]
        if diagonal:
            live = live & (key_pos <= cp * toks + lax.broadcasted_iota(jnp.int32, (rows, toks), 1))
        bias[:rows] = jnp.where(live, 0.0, MASKED)
        for g in range(heads // group):
            columns = slice(g * HEAD_DIM, (g + 1) * HEAD_DIM)
            keys = kv[0, slot, first : first + rows, columns]
            values = kv[1, slot, first : first + rows, columns].T
            for h in range(g * group, (g + 1) * group):
                scores = jnp.dot(keys, qt[h], preferred_element_type=jnp.float32) + bias[:rows]
                old = top[h : h + 1]
                new = jnp.maximum(old, jnp.max(scores, axis=0, keepdims=True))
                weights = jnp.exp2((scores - new) * factor)
                rescale = jnp.exp2((old - new) * factor)
                top[h : h + 1] = new
                total[h : h + 1] = total[h : h + 1] * rescale + jnp.sum(weights, axis=0, keepdims=True)
                acc[h] = acc[h] * rescale + jnp.dot(
                    values, weights.astype(jnp.bfloat16), preferred_element_type=jnp.float32)

    absorb(OWN, 0, cp, diagonal=True)
    absorb(OWN, 1, cp, diagonal=True)

    H = ((0, 1), (2, 3))
    steps0 = ((0, 0), (1, 0), (0, 1), (1, 1), (2, 0), (3, 0), (2, 1), (3, 1), (FAR, 0), (FAR, 1), (4, 0), (5, 0), (4, 1), (5, 1))
    steps1 = ((FAR, 0), (0, 0), (FAR, 1), (0, 1), (1, 0), (2, 0), (1, 1), (2, 1), (3, 0), (3, 1), (4, 0), (5, 0), (4, 1), (5, 1))
    ahead0 = {t: ((slot, H[half]),) for t, (slot, half) in enumerate(steps0)}
    ahead1 = {
        0: ((FAR, H[0]),),
        1: ((1, H[0]), (RELAY, (0,)), (0, H[0])),
        2: ((FAR, H[1]),),
        3: ((RELAY, (1,)), (1, H[1]), (0, H[1])),
        5: ((RELAY, (2,)), (3, H[0]), (2, H[0])),
        7: ((RELAY, (3,)), (LANDED, (0, 1, 2)), (3, H[1]), (LANDED, (3,)), (2, H[1])),
        10: ((5, H[0]), (4, H[0])),
        12: ((5, H[1]), (4, H[1])),
    }
    for t in range(len(steps0)):
        if t in ahead0:
            on(0, *ahead0[t])
        if t in ahead1:
            on(1, *ahead1[t])
        (slot0, half), (slot1, half1) = steps0[t], steps1[t]
        assert half == half1
        slot = slot0 if slot0 == slot1 else jnp.where(core == 0, slot0, slot1)

        def block_of(slot, me):
            if slot == FAR:
                return 2 * chip - 7 if me == 0 else 2 * chip
            return 2 * (chip - slot // 2 - 1) + slot % 2

        absorb(slot, half, jnp.where(core == 0, block_of(slot0, 0), block_of(slot1, 1)))

    stores = []
    for h in range(heads):
        columns = slice(h * HEAD_DIM, (h + 1) * HEAD_DIM)
        out_v[:, columns] = (acc[h] / total[h : h + 1]).T.astype(out_v.dtype)
        if h % group == group - 1:
            columns = pl.ds((h + 1 - group) * HEAD_DIM, group * HEAD_DIM)
            copy = pltpu.make_async_copy(out_v.at[:, columns], out_hbm.at[:, columns], out_sem.at[h // group])
            copy.start()
            stores.append(copy)
    for me in (0, 1):
        @pl.when(core == me)
        def _():
            for p in range(4):
                for lane in own_lanes[me]:
                    own_send(lane, p).wait_send()
                for slot in relayed[me]:
                    relay(slot, p).wait_send()
                for slot in crossed[me]:
                    cross(slot, p).wait_send()
    for copy in stores:
        copy.wait()


def body(count, queries, keys, values, lengths):
    toks, wide = queries.shape
    heads = wide // HEAD_DIM
    return pl.pallas_call(
        functools.partial(kernel, count),
        out_shape=jax.ShapeDtypeStruct((toks, wide), jnp.bfloat16),
        in_specs=[pl.BlockSpec(memory_space=pl.ANY)] * 3 + [pl.BlockSpec(memory_space=pltpu.SMEM)],
        out_specs=pl.BlockSpec(memory_space=pl.ANY),
        scratch_shapes=[
            pltpu.VMEM((2, SLOTS, toks, keys.shape[1]), jnp.bfloat16),
            pltpu.VMEM((toks, wide), jnp.bfloat16),
            pltpu.VMEM((heads, HEAD_DIM, toks), jnp.bfloat16),
            pltpu.VMEM((heads, HEAD_DIM, toks), jnp.float32),
            pltpu.VMEM((heads, toks), jnp.float32),
            pltpu.VMEM((heads, toks), jnp.float32),
            pltpu.VMEM((1, toks), jnp.int32),
            pltpu.VMEM((HALVES[0][1], toks), jnp.float32),
            pltpu.VMEM((toks, wide), jnp.bfloat16),
            pltpu.SemaphoreType.DMA((3,)),
            pltpu.SemaphoreType.DMA((2,)),
            pltpu.SemaphoreType.DMA((SLOTS, 4)),
            pltpu.SemaphoreType.DMA((3, 4)),
            pltpu.SemaphoreType.DMA((SLOTS, 4)),
            pltpu.SemaphoreType.DMA((SLOTS, 4)),
        ],
        compiler_params=pltpu.CompilerParams(collective_id=0, has_side_effects=True),
    )(queries, keys, values, lengths)


def solution(mesh):
    in_specs = (P("cp", "tp"), P("cp", "tp"), P("cp", "tp"), P())
    return jax.shard_map(functools.partial(body, mesh.shape["cp"]), mesh=mesh, in_specs=in_specs,
                         out_specs=P("cp", "tp"), check_vma=False)
```

time: 120 us -> 61.6 us (0.51)
  the two profiles are of different devices: /device:TPU:398 before, /device:TPU:1 now
where the time goes in v1:
time: 61.6 us; the launch traced here: 61.5 us
  Pallas kernels  59.4 us (96%)
  local copies, waits for them, and re-layouts  2.06 us (3%)
    pallas_call x1, Pallas kernels, body(): pl.pallas_call(functools.partial(kernel, count), out_shape=jax.ShapeDtype...  59.4 us
    unnamed x1, local copies, waits for them, and re-layouts  2.06 us

profile of v1, /device:TPU:1, one launch (start us, length us, event | category | flops | bytes accessed | tf_op | source)
XLA Modules:
  0.0 61.5 jit_solution(10616000377846454873)
XLA Ops:
  0.0 59.4 %shard_map.46 = bf16[384,1024]{1,0:T(8,128)(2,1)} custom-call(bf16[384,1024]{1,0:T(8,128)(2,1)} %q_hbm.1, bf16[384,256]{1,0:T(8,128)(2,1)} %k_hbm.1, bf16[384,256]{1,0:T(8,128)(2,1)} %v_hbm.1, s32[32]{0:T(128)} %lengths.1), custom_call_target="tpu_custom_call" | custom-call | tf_op jit(solution)/shard_map/pallas_call | solution.py:216
  59.4 2.1 %copy.6 = bf16[384,1024]{1,0:T(8,128)(2,1)} copy(bf16[384,1024]{1,0:T(8,128)(2,1)} %shard_map.46) | data formatting | bytes 1572864

commit v2 on v1

v2 whole, which is shorter than its diff:
```python
import functools
import math

import jax
import jax.numpy as jnp
from jax import lax
from jax.experimental import pallas as pl
from jax.experimental.pallas import tpu as pltpu
from jax.sharding import PartitionSpec as P

HEAD_DIM = 128
RING_Y = 8
PAIR = 2
MASKED = -1e30
FAR = 6
LANDED = 7
RELAY = 8
OWN = 9
SLOTS = 10
FIRST, SECOND = (0, 1), (2, 3)
STEPS = 16
AHEAD = (
    {2: ((0, FIRST),), 3: ((1, FIRST),), 4: ((0, SECOND),), 5: ((1, SECOND),),
     6: ((2, FIRST),), 7: ((3, FIRST),), 8: ((2, SECOND),), 9: ((3, SECOND),),
     10: ((FAR, FIRST),), 11: ((FAR, SECOND),),
     12: ((4, FIRST),), 13: ((5, FIRST),), 14: ((4, SECOND),), 15: ((5, SECOND),)},
    {2: ((FAR, FIRST),), 3: ((FAR, SECOND),),
     4: ((1, FIRST), (RELAY, (0,)), (0, FIRST)), 6: ((RELAY, (1,)), (1, SECOND), (0, SECOND)),
     8: ((RELAY, (2,)), (3, FIRST), (2, FIRST)),
     10: ((RELAY, (3,)), (LANDED, (0, 1, 2)), (3, SECOND), (LANDED, (3,)), (2, SECOND)),
     12: ((5, FIRST), (4, FIRST)), 14: ((5, SECOND), (4, SECOND))},
)
OWN_LANES = ((0, 1), (0, 2))
RELAYED = ((0, 2), (1, RELAY, LANDED))
CROSSED = ((0, 2, 4), (1, 3, LANDED, 5))


def kernel(count, q_hbm, k_hbm, v_hbm, lengths, out_hbm,
           kv, q_in, qt, acc, top, total, first_live, bias, scores, weights, old_top, new_top, rescale, out_v,
           load_sem, out_sem, recv_sem, own_sem, relay_sem, cross_sem):
    toks = q_in.shape[0]
    kv_heads = kv.shape[2]
    heads = q_in.shape[1] // HEAD_DIM
    group = heads // kv_heads
    factor = HEAD_DIM ** -0.5 * math.log2(math.e)
    cp = lax.axis_index("cp")
    chip, core = cp // 2, lax.rem(cp, 2)
    chips = count // 2
    y = lax.rem(chip, RING_Y)
    row = chip - y

    def core_of(which_chip):
        return which_chip * 2 + core

    partner = chip * 2 + (1 - core)
    has_after, has_before = chip + 1 < chips, chip >= 1
    after, before = core_of(jnp.minimum(chip + 1, chips - 1)), core_of(jnp.maximum(chip - 1, 0))
    three_down = core_of(row + lax.rem(y + RING_Y - 3, RING_Y))
    goes_down = chip + 3 < chips
    relay_owner = row + lax.rem(y + 3, RING_Y)
    three_up = core_of(relay_owner)
    has_relay = relay_owner + 3 < chips
    relay_last = relay_owner + 4 == chips
    relay_to = core_of(jnp.minimum(relay_owner + 4, chips - 1))
    relay_slot = jnp.where(relay_last, 5, LANDED)
    owner = jnp.maximum(chip - 4, 0)
    owner_y = lax.rem(owner, RING_Y)
    relay_from = core_of(owner - owner_y + lax.rem(owner_y + RING_Y - 3, RING_Y))
    has_landed = chip >= 4
    is_last = chip + 1 == chips
    last_from = core_of(chips - 4 - (chips - 4) % RING_Y + ((chips - 4) % RING_Y + RING_Y - 3) % RING_Y)

    def holds(slot, me):
        if slot == RELAY:
            return has_relay
        if slot == LANDED or (slot == FAR and me == 0):
            return has_landed
        if slot == FAR or slot == OWN:
            return chip >= 0
        return chip >= slot // 2 + 1

    def piece(slot, p):
        return kv.at[slot, p % 2, p // 2]

    def remote(src, dst, send, recv, to):
        return pltpu.make_async_remote_copy(
            src_ref=src, dst_ref=dst, send_sem=send, recv_sem=recv,
            device_id={"cp": to}, device_id_type=pl.DeviceIdType.MESH)

    loads = []
    for p in range(4):
        source = (k_hbm, v_hbm)[p % 2].at[:, pl.ds(p // 2 * HEAD_DIM, HEAD_DIM)]
        loads.append(pltpu.make_async_copy(source, piece(OWN, p), load_sem.at[p]))
    loads.append(pltpu.make_async_copy(q_hbm, q_in, load_sem.at[4]))
    for copy in loads:
        copy.start()

    barrier = pltpu.get_barrier_semaphore()

    def greet(peers):
        for known, device in peers:
            @pl.when(known)
            def _():
                pl.semaphore_signal(barrier, inc=1, device_id={"cp": device}, device_id_type=pl.DeviceIdType.MESH)
        pl.semaphore_wait(barrier, sum(known.astype(jnp.int32) for known, _ in peers))

    near = ((chip >= 0, partner), (has_after, after), (has_before, before))

    @pl.when(core == 0)
    def _():
        greet(near)

    @pl.when(core == 1)
    def _():
        greet(near + ((goes_down, three_down), (has_relay, three_up), (has_relay, relay_to),
                      (has_landed, relay_from), (is_last, last_from)))

    for copy in loads[:4]:
        copy.wait()

    def own_send(lane, p):
        to, slot = ((after, core), (partner, FAR), (three_down, RELAY))[lane]
        return (has_after, chip >= 0, goes_down)[lane], remote(
            piece(OWN, p), piece(slot, p), own_sem.at[lane, p], recv_sem.at[slot, p], to)

    def relay(slot, p):
        to, target = {0: (after, 2), 1: (after, 3), 2: (after, 4), RELAY: (relay_to, relay_slot), LANDED: (before, 5)}[slot]
        known = holds(slot, 0) & has_after if slot in (0, 1, 2) else holds(slot, 1)
        return known, remote(piece(slot, p), piece(target, p), relay_sem.at[slot, p], recv_sem.at[target, p], to)

    def cross(slot, p):
        target = FAR if slot == LANDED else slot
        return holds(slot, 1), remote(piece(slot, p), piece(target, p), cross_sem.at[slot, p], recv_sem.at[target, p], partner)

    def if_known(known_and_copy, act):
        known, copy = known_and_copy

        @pl.when(known)
        def _():
            act(copy)

    def event(me, slot, pieces):
        for p in pieces:
            @pl.when(holds(slot, me))
            def _():
                remote(piece(slot, p), piece(slot, p), cross_sem.at[slot, p], recv_sem.at[slot, p], partner).wait_recv()
                if slot in RELAYED[me]:
                    if_known(relay(slot, p), lambda copy: copy.start())
                if slot in CROSSED[me]:
                    cross(slot, p)[1].start()

    for me in (0, 1):
        @pl.when(core == me)
        def _():
            for p in range(4):
                for lane in OWN_LANES[me]:
                    if_known(own_send(lane, p), lambda copy: copy.start())

    for slot in range(FAR + 1):
        @pl.when(~(holds(slot, 1) if slot < FAR else (holds(FAR, 0) | (core == 1))))
        def _():
            kv[slot] = jnp.zeros(kv.shape[1:], kv.dtype)

    query_pos = cp * toks + lax.broadcasted_iota(jnp.int32, (1, toks), 1)
    starts = jnp.zeros((1, toks), jnp.int32)
    position = jnp.int32(0)
    for doc in range(lengths.shape[0]):
        starts = jnp.where(query_pos >= position, position, starts)
        position = position + lengths[doc]
    first_live[...] = starts

    loads[4].wait()
    for h in range(heads):
        qt[h // group, h % group] = q_in[:, h * HEAD_DIM : (h + 1) * HEAD_DIM].T
    acc[...] = jnp.zeros_like(acc)
    total[...] = jnp.zeros_like(total)
    top[...] = jnp.full_like(top, MASKED)
    old_top[...] = jnp.zeros_like(old_top)
    new_top[...] = jnp.zeros_like(new_top)
    rescale[...] = jnp.ones_like(rescale)
    for half in range(2):
        for k in range(PAIR):
            scores[half, k] = jnp.full(scores.shape[2:], MASKED, jnp.float32)
            weights[half, k] = jnp.zeros(weights.shape[2:], weights.dtype)

    def where_is(step):
        in_pairs = jnp.where(core == 0, jnp.where(step < 10, step - 2, step - 4), step - 4)
        far = jnp.where(core == 0, (step == 10) | (step == 11), (step == 2) | (step == 3))
        single = far | (step < 2)
        in_pairs = jnp.maximum(in_pairs, 0)
        distance = in_pairs // 4
        parity = lax.rem(in_pairs, 2)
        slot = jnp.where(step < 2, OWN, jnp.where(far, FAR, 2 * distance + parity))
        head = jnp.where(single, lax.rem(step, 2), lax.rem(in_pairs, 4) // 2)
        far_block = jnp.where(core == 0, 2 * chip - 7, 2 * chip)
        block = jnp.where(step < 2, cp, jnp.where(far, far_block, 2 * (chip - distance - 1) + parity))
        return slot, head, block

    def score(slot, head, half):
        keys = kv[slot, 0, head]
        side = lax.rem(slot, 2)
        for k in range(PAIR):
            h = half * PAIR + k
            found = jnp.dot(keys, qt[head, h], preferred_element_type=jnp.float32) + bias[side]
            scores[half, k] = found
            old = top[head, pl.ds(h, 1)]
            new = jnp.maximum(old, jnp.max(found, axis=0, keepdims=True))
            top[head, pl.ds(h, 1)] = new
            old_top[half, pl.ds(k, 1)] = old
            new_top[half, pl.ds(k, 1)] = new

    def weigh(head, half):
        for k in range(PAIR):
            h = half * PAIR + k
            new = new_top[half, pl.ds(k, 1)]
            shrink = jnp.exp2((old_top[half, pl.ds(k, 1)] - new) * factor)
            found = jnp.exp2((scores[half, k] - new) * factor)
            weights[half, k] = found.astype(jnp.bfloat16)
            rescale[half, pl.ds(k, 1)] = shrink
            total[head, pl.ds(h, 1)] = total[head, pl.ds(h, 1)] * shrink + jnp.sum(found, axis=0, keepdims=True)

    def gather(head, half, values):
        for k in range(PAIR):
            h = half * PAIR + k
            acc[head, h] = acc[head, h] * rescale[half, pl.ds(k, 1)] + jnp.dot(
                values, weights[half, k], preferred_element_type=jnp.float32)

    def step_body(step, carry):
        for quarter in range(STEPS // 4):
            @pl.when(step // 4 == quarter)
            def _():
                for s in range(4 * quarter, 4 * quarter + 4):
                    for me in (0, 1):
                        if s in AHEAD[me]:
                            @pl.when((step == s) & (core == me))
                            def _():
                                for slot, pieces in AHEAD[me][s]:
                                    event(me, slot, pieces)

        slot, head, block = where_is(step)
        last_slot, last_head, _ = where_is(jnp.maximum(step - 1, 0))

        @pl.when(head == 0)
        def _():
            key_pos = block * toks + lax.broadcasted_iota(jnp.int32, (toks, toks), 0)
            live = (key_pos >= first_live[...]) & (key_pos <= cp * toks + lax.broadcasted_iota(jnp.int32, (toks, toks), 1))
            bias[lax.rem(slot, 2)] = jnp.where(live, 0.0, MASKED)

        values = kv[last_slot, 1, last_head].T
        score(slot, head, 0)
        weigh(last_head, 1)
        gather(last_head, 0, values)
        score(slot, head, 1)
        weigh(head, 0)
        gather(last_head, 1, values)
        return carry

    lax.fori_loop(0, STEPS, step_body, 0)
    last_slot, last_head, _ = where_is(jnp.int32(STEPS - 1))
    values = kv[last_slot, 1, last_head].T
    weigh(last_head, 1)
    gather(last_head, 0, values)
    gather(last_head, 1, values)

    stores = []
    for h in range(heads):
        columns = slice(h * HEAD_DIM, (h + 1) * HEAD_DIM)
        share = 1.0 / total[h // group, h % group : h % group + 1]
        out_v[:, columns] = (acc[h // group, h % group] * share).astype(out_v.dtype).T
        if h % group == group - 1:
            columns = pl.ds((h + 1 - group) * HEAD_DIM, group * HEAD_DIM)
            copy = pltpu.make_async_copy(out_v.at[:, columns], out_hbm.at[:, columns], out_sem.at[h // group])
            copy.start()
            stores.append(copy)
    for me in (0, 1):
        @pl.when(core == me)
        def _():
            for p in range(4):
                for lane in OWN_LANES[me]:
                    if_known(own_send(lane, p), lambda copy: copy.wait_send())
                for slot in RELAYED[me]:
                    if_known(relay(slot, p), lambda copy: copy.wait_send())
                for slot in CROSSED[me]:
                    if_known(cross(slot, p), lambda copy: copy.wait_send())
    for copy in stores:
        copy.wait()


def body(count, queries, keys, values, lengths):
    toks, wide = queries.shape
    heads = wide // HEAD_DIM
    kv_heads = keys.shape[1] // HEAD_DIM
    group = heads // kv_heads
    return pl.pallas_call(
        functools.partial(kernel, count),
        out_shape=jax.ShapeDtypeStruct((toks, wide), jnp.bfloat16),
        in_specs=[pl.BlockSpec(memory_space=pl.ANY)] * 3 + [pl.BlockSpec(memory_space=pltpu.SMEM)],
        out_specs=pl.BlockSpec(memory_space=pl.ANY),
        scratch_shapes=[
            pltpu.VMEM((SLOTS, 2, kv_heads, toks, HEAD_DIM), jnp.bfloat16),
            pltpu.VMEM((toks, wide), jnp.bfloat16),
            pltpu.VMEM((kv_heads, group, HEAD_DIM, toks), jnp.bfloat16),
            pltpu.VMEM((kv_heads, group, HEAD_DIM, toks), jnp.float32),
            pltpu.VMEM((kv_heads, group, toks), jnp.float32),
            pltpu.VMEM((kv_heads, group, toks), jnp.float32),
            pltpu.VMEM((1, toks), jnp.int32),
            pltpu.VMEM((2, toks, toks), jnp.float32),
            pltpu.VMEM((2, PAIR, toks, toks), jnp.float32),
            pltpu.VMEM((2, PAIR, toks, toks), jnp.bfloat16),
            pltpu.VMEM((2, PAIR, toks), jnp.float32),
            pltpu.VMEM((2, PAIR, toks), jnp.float32),
            pltpu.VMEM((2, PAIR, toks), jnp.float32),
            pltpu.VMEM((toks, wide), jnp.bfloat16),
            pltpu.SemaphoreType.DMA((5,)),
            pltpu.SemaphoreType.DMA((2,)),
            pltpu.SemaphoreType.DMA((SLOTS, 4)),
            pltpu.SemaphoreType.DMA((3, 4)),
            pltpu.SemaphoreType.DMA((SLOTS, 4)),
            pltpu.SemaphoreType.DMA((SLOTS, 4)),
        ],
        compiler_params=pltpu.CompilerParams(collective_id=0, has_side_effects=True),
    )(queries, keys, values, lengths)


def solution(mesh):
    in_specs = (P("cp", "tp"), P("cp", "tp"), P("cp", "tp"), P())
    return jax.shard_map(functools.partial(body, mesh.shape["cp"]), mesh=mesh, in_specs=in_specs,
                         out_specs=P("cp", "tp"), check_vma=False)
```

time: 61.6 us -> 45.2 us (0.73)
  the two profiles are of different devices: /device:TPU:1 before, /device:TPU:387 now
where the time goes in v2:
time: 45.2 us; the launch traced here: 45.1 us
  Pallas kernels  43 us (95%)
  local copies, waits for them, and re-layouts  2.06 us (5%)
    pallas_call x1, Pallas kernels, body(): pl.pallas_call(functools.partial(kernel, count), out_shape=jax.ShapeDtype...  43 us
    unnamed x1, local copies, waits for them, and re-layouts  2.06 us

profile of v2, /device:TPU:387, one launch (start us, length us, event | category | flops | bytes accessed | tf_op | source)
XLA Modules:
  0.0 45.1 jit_solution(5870848730557562660)
XLA Ops:
  0.0 43.0 %shard_map.46 = bf16[384,1024]{1,0:T(8,128)(2,1)} custom-call(bf16[384,1024]{1,0:T(8,128)(2,1)} %q_hbm.1, bf16[384,256]{1,0:T(8,128)(2,1)} %k_hbm.1, bf16[384,256]{1,0:T(8,128)(2,1)} %v_hbm.1, s32[32]{0:T(128)} %lengths.1), custom_call_target="tpu_custom_call" | custom-call | tf_op jit(solution)/shard_map/pallas_call | solution.py:294
  43.0 2.1 %copy.6 = bf16[384,1024]{1,0:T(8,128)(2,1)} copy(bf16[384,1024]{1,0:T(8,128)(2,1)} %shard_map.46) | data formatting | bytes 1572864

commit v3 on v2

--- a/solution.py
+++ b/solution.py
@@ -16,27 +16,29 @@
 LANDED = 7
 RELAY = 8
 OWN = 9
-SLOTS = 10
+SPARE = 10
+SLOTS = 11
 FIRST, SECOND = (0, 1), (2, 3)
-STEPS = 16
+STEPS = 14
+SHORT_WAY = (3,)
 AHEAD = (
-    {2: ((0, FIRST),), 3: ((1, FIRST),), 4: ((0, SECOND),), 5: ((1, SECOND),),
-     6: ((2, FIRST),), 7: ((3, FIRST),), 8: ((2, SECOND),), 9: ((3, SECOND),),
-     10: ((FAR, FIRST),), 11: ((FAR, SECOND),),
-     12: ((4, FIRST),), 13: ((5, FIRST),), 14: ((4, SECOND),), 15: ((5, SECOND),)},
-    {2: ((FAR, FIRST),), 3: ((FAR, SECOND),),
-     4: ((1, FIRST), (RELAY, (0,)), (0, FIRST)), 6: ((RELAY, (1,)), (1, SECOND), (0, SECOND)),
-     8: ((RELAY, (2,)), (3, FIRST), (2, FIRST)),
-     10: ((RELAY, (3,)), (LANDED, (0, 1, 2)), (3, SECOND), (LANDED, (3,)), (2, SECOND)),
-     12: ((5, FIRST), (4, FIRST)), 14: ((5, SECOND), (4, SECOND))},
+    {0: ((0, FIRST),), 1: ((1, FIRST),), 2: ((0, SECOND),), 3: ((1, SECOND),),
+     4: ((2, FIRST),), 5: ((3, FIRST),), 6: ((2, SECOND),), 7: ((3, SECOND),),
+     8: ((FAR, FIRST),), 9: ((FAR, SECOND),),
+     10: ((4, FIRST),), 11: ((5, FIRST),), 12: ((4, SECOND),), 13: ((5, SECOND),)},
+    {0: ((FAR, FIRST),), 1: ((FAR, SECOND),),
+     2: ((1, FIRST), (RELAY, (0,)), (SPARE, (0,)), (0, FIRST)), 4: ((RELAY, (1,)), (SPARE, (1,)), (1, SECOND), (0, SECOND)),
+     6: ((RELAY, (2,)), (SPARE, (2, 3)), (3, FIRST), (2, FIRST)),
+     8: ((RELAY, (3,)), (LANDED, (0, 1)), (3, SECOND), (LANDED, (2, 3)), (2, SECOND)),
+     10: ((5, FIRST), (4, FIRST)), 12: ((5, SECOND), (4, SECOND))},
 )
-OWN_LANES = ((0, 1), (0, 2))
-RELAYED = ((0, 2), (1, RELAY, LANDED))
+OWN_LANES = ((0, 1), (0, 2, 3))
+RELAYED = ((0, 2), (1, 3, RELAY, LANDED, SPARE))
 CROSSED = ((0, 2, 4), (1, 3, LANDED, 5))
 
 
 def kernel(count, q_hbm, k_hbm, v_hbm, lengths, out_hbm,
-           kv, q_in, qt, acc, top, total, first_live, bias, scores, weights, old_top, new_top, rescale, out_v,
+           kv, q_in, qt, acc, top, total, bounds, key_mask, query_mask, scores, weights, old_top, new_top, rescale, out_v,
            load_sem, out_sem, recv_sem, own_sem, relay_sem, cross_sem):
     toks = q_in.shape[0]
     kv_heads = kv.shape[2]
@@ -55,24 +57,22 @@
     partner = chip * 2 + (1 - core)
     has_after, has_before = chip + 1 < chips, chip >= 1
     after, before = core_of(jnp.minimum(chip + 1, chips - 1)), core_of(jnp.maximum(chip - 1, 0))
-    three_down = core_of(row + lax.rem(y + RING_Y - 3, RING_Y))
-    goes_down = chip + 3 < chips
-    relay_owner = row + lax.rem(y + 3, RING_Y)
-    three_up = core_of(relay_owner)
-    has_relay = relay_owner + 3 < chips
-    relay_last = relay_owner + 4 == chips
-    relay_to = core_of(jnp.minimum(relay_owner + 4, chips - 1))
-    relay_slot = jnp.where(relay_last, 5, LANDED)
-    owner = jnp.maximum(chip - 4, 0)
-    owner_y = lax.rem(owner, RING_Y)
-    relay_from = core_of(owner - owner_y + lax.rem(owner_y + RING_Y - 3, RING_Y))
+    goes_down = chip + 4 < chips
+    down = core_of(jnp.minimum(row + jnp.where(y >= 4, RING_Y, 0), chips - RING_Y) + lax.rem(y + RING_Y - 3, RING_Y))
+    reader = row + lax.rem(y + RING_Y - 1, RING_Y)
+    has_relay = reader >= 4
+    relay_to, relay_owner = core_of(reader), core_of(jnp.maximum(reader - 4, 0))
+    relay_from = core_of(row + lax.rem(y + 1, RING_Y))
     has_landed = chip >= 4
-    is_last = chip + 1 == chips
-    last_from = core_of(chips - 4 - (chips - 4) % RING_Y + ((chips - 4) % RING_Y + RING_Y - 3) % RING_Y)
+    owner_chip, reader_chip = chips - 4, chips - 1
+    between_chip = owner_chip - owner_chip % RING_Y + (owner_chip + RING_Y - 3) % RING_Y
+    is_owner, is_between, is_reader = chip == owner_chip, chip == between_chip, chip == reader_chip
 
     def holds(slot, me):
         if slot == RELAY:
             return has_relay
+        if slot == SPARE:
+            return is_between
         if slot == LANDED or (slot == FAR and me == 0):
             return has_landed
         if slot == FAR or slot == OWN:
@@ -112,21 +112,30 @@
 
     @pl.when(core == 1)
     def _():
-        greet(near + ((goes_down, three_down), (has_relay, three_up), (has_relay, relay_to),
-                      (has_landed, relay_from), (is_last, last_from)))
+        greet(near + ((goes_down, down), (has_relay, relay_owner), (has_relay, relay_to), (has_landed, relay_from),
+                      (is_owner | is_reader, core_of(between_chip)),
+                      (is_between, core_of(owner_chip)), (is_between, core_of(reader_chip))))
 
     for copy in loads[:4]:
         copy.wait()
 
     def own_send(lane, p):
-        to, slot = ((after, core), (partner, FAR), (three_down, RELAY))[lane]
-        return (has_after, chip >= 0, goes_down)[lane], remote(
+        to, slot = ((after, core), (partner, FAR), (down, RELAY), (core_of(between_chip), SPARE))[lane]
+        return (has_after, chip >= 0, goes_down, is_owner)[lane], remote(
             piece(OWN, p), piece(slot, p), own_sem.at[lane, p], recv_sem.at[slot, p], to)
 
     def relay(slot, p):
-        to, target = {0: (after, 2), 1: (after, 3), 2: (after, 4), RELAY: (relay_to, relay_slot), LANDED: (before, 5)}[slot]
-        known = holds(slot, 0) & has_after if slot in (0, 1, 2) else holds(slot, 1)
+        to, target = {0: (after, 2), 1: (after, 3), 2: (after, 4), 3: (after, 5),
+                      RELAY: (relay_to, LANDED), LANDED: (before, 5), SPARE: (core_of(reader_chip), 5)}[slot]
+        known = holds(slot, 1)
+        if slot < FAR:
+            known = known & has_after
         return known, remote(piece(slot, p), piece(target, p), relay_sem.at[slot, p], recv_sem.at[target, p], to)
+
+    def relayed(me, slot, p):
+        if slot == 3 and p not in SHORT_WAY or slot in (LANDED, SPARE) and p in SHORT_WAY:
+            return False
+        return slot in RELAYED[me]
 
     def cross(slot, p):
         target = FAR if slot == LANDED else slot
@@ -144,7 +153,7 @@
             @pl.when(holds(slot, me))
             def _():
                 remote(piece(slot, p), piece(slot, p), cross_sem.at[slot, p], recv_sem.at[slot, p], partner).wait_recv()
-                if slot in RELAYED[me]:
+                if relayed(me, slot, p):
                     if_known(relay(slot, p), lambda copy: copy.start())
                 if slot in CROSSED[me]:
                     cross(slot, p)[1].start()
@@ -161,39 +170,73 @@
         def _():
             kv[slot] = jnp.zeros(kv.shape[1:], kv.dtype)
 
-    query_pos = cp * toks + lax.broadcasted_iota(jnp.int32, (1, toks), 1)
-    starts = jnp.zeros((1, toks), jnp.int32)
+    feature = lax.broadcasted_iota(jnp.int32, (1, HEAD_DIM), 1)
+    begins = jnp.where(feature == lengths.shape[0], -(1 << 20), jnp.full((1, HEAD_DIM), 1 << 20, jnp.int32))
+    ends = jnp.zeros((1, HEAD_DIM), jnp.int32)
     position = jnp.int32(0)
     for doc in range(lengths.shape[0]):
-        starts = jnp.where(query_pos >= position, position, starts)
+        begins = jnp.where(feature == doc, position, begins)
         position = position + lengths[doc]
-    first_live[...] = starts
+        ends = jnp.where(feature == doc, position, ends)
+    bounds[0:1] = begins.astype(jnp.float32)
+    bounds[1:2] = ends.astype(jnp.float32)
+    begins = jnp.broadcast_to(bounds[0:1], (HEAD_DIM, HEAD_DIM)).T
+    ends = jnp.broadcast_to(bounds[1:2], (HEAD_DIM, HEAD_DIM)).T
+    for tile in range(toks // HEAD_DIM):
+        query_pos = (cp * toks + tile * HEAD_DIM + lax.broadcasted_iota(jnp.int32, (HEAD_DIM, HEAD_DIM), 1)).astype(jnp.float32)
+        outside = (query_pos < begins) | (query_pos >= ends)
+        outside = outside & (lax.broadcasted_iota(jnp.int32, (HEAD_DIM, HEAD_DIM), 0) <= lengths.shape[0])
+        query_mask[:, tile * HEAD_DIM : (tile + 1) * HEAD_DIM] = jnp.where(outside, MASKED, 0.0).astype(jnp.bfloat16)
+
+    def mark(side, block):
+        key_pos = (block * toks + lax.broadcasted_iota(jnp.int32, (toks, HEAD_DIM), 0)).astype(jnp.float32)
+        inside = (key_pos >= bounds[0:1]) & (key_pos < bounds[1:2])
+        key_mask[side] = jnp.where(inside, 1.0, 0.0).astype(jnp.bfloat16)
+
+    def product(keys, side, head, h):
+        return jnp.dot(
+            jnp.concatenate([keys, key_mask[side]], axis=1),
+            jnp.concatenate([qt[head, h], query_mask[...]], axis=0),
+            preferred_element_type=jnp.float32)
 
     loads[4].wait()
     for h in range(heads):
         qt[h // group, h % group] = q_in[:, h * HEAD_DIM : (h + 1) * HEAD_DIM].T
-    acc[...] = jnp.zeros_like(acc)
-    total[...] = jnp.zeros_like(total)
-    top[...] = jnp.full_like(top, MASKED)
     old_top[...] = jnp.zeros_like(old_top)
     new_top[...] = jnp.zeros_like(new_top)
     rescale[...] = jnp.ones_like(rescale)
-    for half in range(2):
-        for k in range(PAIR):
-            scores[half, k] = jnp.full(scores.shape[2:], MASKED, jnp.float32)
+    for k in range(PAIR):
+        scores[1, k] = jnp.full(scores.shape[2:], MASKED, jnp.float32)
+        for half in range(2):
             weights[half, k] = jnp.zeros(weights.shape[2:], weights.dtype)
 
+    mark(1, cp)
+
+    def own_body(head, carry):
+        keys = kv[OWN, 0, head]
+        values = kv[OWN, 1, head].T
+        causal = lax.broadcasted_iota(jnp.int32, (toks, toks), 0) <= lax.broadcasted_iota(jnp.int32, (toks, toks), 1)
+        for h in range(group):
+            found = jnp.where(causal, product(keys, 1, head, h), MASKED)
+            new = jnp.max(found, axis=0, keepdims=True)
+            found = jnp.exp2((found - new) * factor)
+            top[head, pl.ds(h, 1)] = new
+            total[head, pl.ds(h, 1)] = jnp.sum(found, axis=0, keepdims=True)
+            acc[head, h] = jnp.dot(values, found.astype(jnp.bfloat16), preferred_element_type=jnp.float32)
+        return carry
+
+    lax.fori_loop(0, kv_heads, own_body, 0)
+
     def where_is(step):
-        in_pairs = jnp.where(core == 0, jnp.where(step < 10, step - 2, step - 4), step - 4)
-        far = jnp.where(core == 0, (step == 10) | (step == 11), (step == 2) | (step == 3))
-        single = far | (step < 2)
+        in_pairs = jnp.where(core == 0, jnp.where(step < 8, step, step - 2), step - 2)
+        far = jnp.where(core == 0, (step == 8) | (step == 9), step < 2)
         in_pairs = jnp.maximum(in_pairs, 0)
         distance = in_pairs // 4
         parity = lax.rem(in_pairs, 2)
-        slot = jnp.where(step < 2, OWN, jnp.where(far, FAR, 2 * distance + parity))
-        head = jnp.where(single, lax.rem(step, 2), lax.rem(in_pairs, 4) // 2)
+        slot = jnp.where(far, FAR, 2 * distance + parity)
+        head = jnp.where(far, lax.rem(step, 2), lax.rem(in_pairs, 4) // 2)
         far_block = jnp.where(core == 0, 2 * chip - 7, 2 * chip)
-        block = jnp.where(step < 2, cp, jnp.where(far, far_block, 2 * (chip - distance - 1) + parity))
+        block = jnp.where(far, far_block, 2 * (chip - distance - 1) + parity)
         return slot, head, block
 
     def score(slot, head, half):
@@ -201,7 +244,7 @@
         side = lax.rem(slot, 2)
         for k in range(PAIR):
             h = half * PAIR + k
-            found = jnp.dot(keys, qt[head, h], preferred_element_type=jnp.float32) + bias[side]
+            found = product(keys, side, head, h)
             scores[half, k] = found
             old = top[head, pl.ds(h, 1)]
             new = jnp.maximum(old, jnp.max(found, axis=0, keepdims=True))
@@ -226,7 +269,7 @@
                 values, weights[half, k], preferred_element_type=jnp.float32)
 
     def step_body(step, carry):
-        for quarter in range(STEPS // 4):
+        for quarter in range((STEPS + 3) // 4):
             @pl.when(step // 4 == quarter)
             def _():
                 for s in range(4 * quarter, 4 * quarter + 4):
@@ -242,17 +285,15 @@
 
         @pl.when(head == 0)
         def _():
-            key_pos = block * toks + lax.broadcasted_iota(jnp.int32, (toks, toks), 0)
-            live = (key_pos >= first_live[...]) & (key_pos <= cp * toks + lax.broadcasted_iota(jnp.int32, (toks, toks), 1))
-            bias[lax.rem(slot, 2)] = jnp.where(live, 0.0, MASKED)
+            mark(lax.rem(slot, 2), block)
 
         values = kv[last_slot, 1, last_head].T
+        weigh(last_head, 1)
         score(slot, head, 0)
-        weigh(last_head, 1)
         gather(last_head, 0, values)
         score(slot, head, 1)
+        gather(last_head, 1, values)
         weigh(head, 0)
-        gather(last_head, 1, values)
         return carry
 
     lax.fori_loop(0, STEPS, step_body, 0)
@@ -279,7 +320,8 @@
                 for lane in OWN_LANES[me]:
                     if_known(own_send(lane, p), lambda copy: copy.wait_send())
                 for slot in RELAYED[me]:
-                    if_known(relay(slot, p), lambda copy: copy.wait_send())
+                    if relayed(me, slot, p):
+                        if_known(relay(slot, p), lambda copy: copy.wait_send())
                 for slot in CROSSED[me]:
                     if_known(cross(slot, p), lambda copy: copy.wait_send())
     for copy in stores:
@@ -303,8 +345,9 @@
             pltpu.VMEM((kv_heads, group, HEAD_DIM, toks), jnp.float32),
             pltpu.VMEM((kv_heads, group, toks), jnp.float32),
             pltpu.VMEM((kv_heads, group, toks), jnp.float32),
-            pltpu.VMEM((1, toks), jnp.int32),
-            pltpu.VMEM((2, toks, toks), jnp.float32),
+            pltpu.VMEM((2, HEAD_DIM), jnp.float32),
+            pltpu.VMEM((2, toks, HEAD_DIM), jnp.bfloat16),
+            pltpu.VMEM((HEAD_DIM, toks), jnp.bfloat16),
             pltpu.VMEM((2, PAIR, toks, toks), jnp.float32),
             pltpu.VMEM((2, PAIR, toks, toks), jnp.bfloat16),
             pltpu.VMEM((2, PAIR, toks), jnp.float32),
@@ -314,7 +357,7 @@
             pltpu.SemaphoreType.DMA((5,)),
             pltpu.SemaphoreType.DMA((2,)),
             pltpu.SemaphoreType.DMA((SLOTS, 4)),
-            pltpu.SemaphoreType.DMA((3, 4)),
+            pltpu.SemaphoreType.DMA((4, 4)),
             pltpu.SemaphoreType.DMA((SLOTS, 4)),
             pltpu.SemaphoreType.DMA((SLOTS, 4)),
         ],

time: 45.2 us -> 42.6 us (0.942)
  the two profiles are of different devices: /device:TPU:387 before, /device:TPU:249 now
where the time goes in v3:
time: 42.6 us; the launch traced here: 42.4 us
  Pallas kernels  40.3 us (95%)
  local copies, waits for them, and re-layouts  2.06 us (5%)
    pallas_call x1, Pallas kernels, body(): pl.pallas_call(functools.partial(kernel, count), out_shape=jax.ShapeDtype...  40.3 us
    unnamed x1, local copies, waits for them, and re-layouts  2.06 us

profile of v3, /device:TPU:249, one launch (start us, length us, event | category | flops | bytes accessed | tf_op | source)
XLA Modules:
  0.0 42.4 jit_solution(2454803929835405637)
XLA Ops:
  0.0 40.3 %shard_map.46 = bf16[384,1024]{1,0:T(8,128)(2,1)} custom-call(bf16[384,1024]{1,0:T(8,128)(2,1)} %q_hbm.1, bf16[384,256]{1,0:T(8,128)(2,1)} %k_hbm.1, bf16[384,256]{1,0:T(8,128)(2,1)} %v_hbm.1, s32[32]{0:T(128)} %lengths.1), custom_call_target="tpu_custom_call" | custom-call | tf_op jit(solution)/shard_map/pallas_call | solution.py:336
  40.3 2.1 %copy.6 = bf16[384,1024]{1,0:T(8,128)(2,1)} copy(bf16[384,1024]{1,0:T(8,128)(2,1)} %shard_map.46) | data formatting | bytes 1572864

commit v4 on v3

--- a/solution.py
+++ b/solution.py
@@ -12,6 +12,7 @@
 RING_Y = 8
 PAIR = 2
 MASKED = -1e30
+TILE = 256
 FAR = 6
 LANDED = 7
 RELAY = 8
@@ -20,26 +21,27 @@
 SLOTS = 11
 FIRST, SECOND = (0, 1), (2, 3)
 STEPS = 14
-SHORT_WAY = (3,)
+SHORT_WAY = (2, 3)
 AHEAD = (
     {0: ((0, FIRST),), 1: ((1, FIRST),), 2: ((0, SECOND),), 3: ((1, SECOND),),
      4: ((2, FIRST),), 5: ((3, FIRST),), 6: ((2, SECOND),), 7: ((3, SECOND),),
      8: ((FAR, FIRST),), 9: ((FAR, SECOND),),
-     10: ((4, FIRST),), 11: ((5, FIRST),), 12: ((4, SECOND),), 13: ((5, SECOND),)},
+     10: ((4, (0,)), (5, FIRST)), 11: ((4, (1,)),), 12: ((5, SECOND), (4, (2,))), 13: ((4, (3,)),)},
     {0: ((FAR, FIRST),), 1: ((FAR, SECOND),),
-     2: ((1, FIRST), (RELAY, (0,)), (SPARE, (0,)), (0, FIRST)), 4: ((RELAY, (1,)), (SPARE, (1,)), (1, SECOND), (0, SECOND)),
+     2: ((1, FIRST), (RELAY, (0,)), (SPARE, (0,)), (0, FIRST)),
+     4: ((RELAY, (1,)), (SPARE, (1,)), (1, SECOND), (0, SECOND)),
      6: ((RELAY, (2,)), (SPARE, (2, 3)), (3, FIRST), (2, FIRST)),
-     8: ((RELAY, (3,)), (LANDED, (0, 1)), (3, SECOND), (LANDED, (2, 3)), (2, SECOND)),
-     10: ((5, FIRST), (4, FIRST)), 12: ((5, SECOND), (4, SECOND))},
+     8: ((RELAY, (3,)), (LANDED, (0, 1)), (3, (2,)), (LANDED, (2,)), (3, (3,)), (LANDED, (3,)), (2, SECOND)),
+     10: ((5, (0,)), (5, (2,)), (5, (1,))), 11: ((5, (3,)), (4, FIRST)), 13: ((4, SECOND),)},
 )
 OWN_LANES = ((0, 1), (0, 2, 3))
 RELAYED = ((0, 2), (1, 3, RELAY, LANDED, SPARE))
 CROSSED = ((0, 2, 4), (1, 3, LANDED, 5))
 
 
-def kernel(count, q_hbm, k_hbm, v_hbm, lengths, out_hbm,
-           kv, q_in, qt, acc, top, total, bounds, key_mask, query_mask, scores, weights, old_top, new_top, rescale, out_v,
-           load_sem, out_sem, recv_sem, own_sem, relay_sem, cross_sem):
+def kernel(count, q_hbm, k_hbm, v_hbm, lengths, out,
+           kv, q_in, qt, acc, top, total, bounds, key_mask, query_mask, scores, weights, old_top, new_top, rescale,
+           load_sem, recv_sem, own_sem, relay_sem, cross_sem):
     toks = q_in.shape[0]
     kv_heads = kv.shape[2]
     heads = q_in.shape[1] // HEAD_DIM
@@ -186,29 +188,32 @@
         query_pos = (cp * toks + tile * HEAD_DIM + lax.broadcasted_iota(jnp.int32, (HEAD_DIM, HEAD_DIM), 1)).astype(jnp.float32)
         outside = (query_pos < begins) | (query_pos >= ends)
         outside = outside & (lax.broadcasted_iota(jnp.int32, (HEAD_DIM, HEAD_DIM), 0) <= lengths.shape[0])
-        query_mask[:, tile * HEAD_DIM : (tile + 1) * HEAD_DIM] = jnp.where(outside, MASKED, 0.0).astype(jnp.bfloat16)
+        for k in range(PAIR):
+            first = k * toks + tile * HEAD_DIM
+            query_mask[:, first : first + HEAD_DIM] = jnp.where(outside, MASKED, 0.0).astype(jnp.bfloat16)
 
     def mark(side, block):
         key_pos = (block * toks + lax.broadcasted_iota(jnp.int32, (toks, HEAD_DIM), 0)).astype(jnp.float32)
         inside = (key_pos >= bounds[0:1]) & (key_pos < bounds[1:2])
         key_mask[side] = jnp.where(inside, 1.0, 0.0).astype(jnp.bfloat16)
 
-    def product(keys, side, head, h):
+    def product(keys, side, head, half, cut=slice(None)):
         return jnp.dot(
             jnp.concatenate([keys, key_mask[side]], axis=1),
-            jnp.concatenate([qt[head, h], query_mask[...]], axis=0),
+            jnp.concatenate([qt[head, half, :, cut], query_mask[:, cut]], axis=0),
             preferred_element_type=jnp.float32)
+
+    cuts = [slice(first, first + TILE) for first in range(0, PAIR * toks, TILE)]
 
     loads[4].wait()
     for h in range(heads):
-        qt[h // group, h % group] = q_in[:, h * HEAD_DIM : (h + 1) * HEAD_DIM].T
+        g, half, k = h // group, h % group // PAIR, h % PAIR
+        qt[g, half, :, k * toks : (k + 1) * toks] = q_in[:, h * HEAD_DIM : (h + 1) * HEAD_DIM].T
     old_top[...] = jnp.zeros_like(old_top)
     new_top[...] = jnp.zeros_like(new_top)
     rescale[...] = jnp.ones_like(rescale)
-    for k in range(PAIR):
-        scores[1, k] = jnp.full(scores.shape[2:], MASKED, jnp.float32)
-        for half in range(2):
-            weights[half, k] = jnp.zeros(weights.shape[2:], weights.dtype)
+    scores[1] = jnp.full(scores.shape[1:], MASKED, jnp.float32)
+    weights[...] = jnp.zeros_like(weights)
 
     mark(1, cp)
 
@@ -216,13 +221,15 @@
         keys = kv[OWN, 0, head]
         values = kv[OWN, 1, head].T
         causal = lax.broadcasted_iota(jnp.int32, (toks, toks), 0) <= lax.broadcasted_iota(jnp.int32, (toks, toks), 1)
-        for h in range(group):
-            found = jnp.where(causal, product(keys, 1, head, h), MASKED)
+        for half in range(group // PAIR):
+            found = product(keys, 1, head, half)
+            found = jnp.concatenate(
+                [jnp.where(causal, found[:, k * toks : (k + 1) * toks], MASKED) for k in range(PAIR)], axis=1)
             new = jnp.max(found, axis=0, keepdims=True)
             found = jnp.exp2((found - new) * factor)
-            top[head, pl.ds(h, 1)] = new
-            total[head, pl.ds(h, 1)] = jnp.sum(found, axis=0, keepdims=True)
-            acc[head, h] = jnp.dot(values, found.astype(jnp.bfloat16), preferred_element_type=jnp.float32)
+            top[head, half] = new
+            total[head, half] = jnp.sum(found, axis=0, keepdims=True)
+            acc[head, half] = jnp.dot(values, found.astype(jnp.bfloat16), preferred_element_type=jnp.float32)
         return carry
 
     lax.fori_loop(0, kv_heads, own_body, 0)
@@ -232,7 +239,7 @@
         far = jnp.where(core == 0, (step == 8) | (step == 9), step < 2)
         in_pairs = jnp.maximum(in_pairs, 0)
         distance = in_pairs // 4
-        parity = lax.rem(in_pairs, 2)
+        parity = lax.rem(in_pairs + step // 10, 2)
         slot = jnp.where(far, FAR, 2 * distance + parity)
         head = jnp.where(far, lax.rem(step, 2), lax.rem(in_pairs, 4) // 2)
         far_block = jnp.where(core == 0, 2 * chip - 7, 2 * chip)
@@ -240,35 +247,42 @@
         return slot, head, block
 
     def score(slot, head, half):
-        keys = kv[slot, 0, head]
-        side = lax.rem(slot, 2)
-        for k in range(PAIR):
-            h = half * PAIR + k
-            found = product(keys, side, head, h)
-            scores[half, k] = found
-            old = top[head, pl.ds(h, 1)]
+        keys, side = kv[slot, 0, head], lax.rem(slot, 2)
+        for cut in cuts:
+            found = product(keys, side, head, half, cut)
+            scores[half, :, cut] = found
+            old = top[head, half, :, cut]
             new = jnp.maximum(old, jnp.max(found, axis=0, keepdims=True))
-            top[head, pl.ds(h, 1)] = new
-            old_top[half, pl.ds(k, 1)] = old
-            new_top[half, pl.ds(k, 1)] = new
+            top[head, half, :, cut] = new
+            old_top[half, :, cut] = old
+            new_top[half, :, cut] = new
 
     def weigh(head, half):
-        for k in range(PAIR):
-            h = half * PAIR + k
-            new = new_top[half, pl.ds(k, 1)]
-            shrink = jnp.exp2((old_top[half, pl.ds(k, 1)] - new) * factor)
-            found = jnp.exp2((scores[half, k] - new) * factor)
-            weights[half, k] = found.astype(jnp.bfloat16)
-            rescale[half, pl.ds(k, 1)] = shrink
-            total[head, pl.ds(h, 1)] = total[head, pl.ds(h, 1)] * shrink + jnp.sum(found, axis=0, keepdims=True)
+        for cut in cuts:
+            new = new_top[half, :, cut]
+            shrink = jnp.exp2((old_top[half, :, cut] - new) * factor)
+            found = jnp.exp2((scores[half, :, cut] - new) * factor)
+            weights[half, :, cut] = found.astype(jnp.bfloat16)
+            rescale[half, :, cut] = shrink
+            total[head, half, :, cut] = total[head, half, :, cut] * shrink + jnp.sum(found, axis=0, keepdims=True)
 
     def gather(head, half, values):
-        for k in range(PAIR):
-            h = half * PAIR + k
-            acc[head, h] = acc[head, h] * rescale[half, pl.ds(k, 1)] + jnp.dot(
-                values, weights[half, k], preferred_element_type=jnp.float32)
+        for cut in cuts:
+            acc[head, half, :, cut] = acc[head, half, :, cut] * rescale[half, :, cut] + jnp.dot(
+                values, weights[half, :, cut], preferred_element_type=jnp.float32)
+
+    def finish(head):
+        for h in range(group):
+            half, cut = h // PAIR, slice(h % PAIR * toks, (h % PAIR + 1) * toks)
+            first = (head * group + h) * HEAD_DIM
+            share = 1.0 / total[head, half, :, cut]
+            out[:, first : first + HEAD_DIM] = (acc[head, half, :, cut] * share).astype(out.dtype).T
 
     def step_body(step, carry):
+        @pl.when(step == STEPS - 1)
+        def _():
+            finish(0)
+
         for quarter in range((STEPS + 3) // 4):
             @pl.when(step // 4 == quarter)
             def _():
@@ -303,16 +317,7 @@
     gather(last_head, 0, values)
     gather(last_head, 1, values)
 
-    stores = []
-    for h in range(heads):
-        columns = slice(h * HEAD_DIM, (h + 1) * HEAD_DIM)
-        share = 1.0 / total[h // group, h % group : h % group + 1]
-        out_v[:, columns] = (acc[h // group, h % group] * share).astype(out_v.dtype).T
-        if h % group == group - 1:
-            columns = pl.ds((h + 1 - group) * HEAD_DIM, group * HEAD_DIM)
-            copy = pltpu.make_async_copy(out_v.at[:, columns], out_hbm.at[:, columns], out_sem.at[h // group])
-            copy.start()
-            stores.append(copy)
+    finish(kv_heads - 1)
     for me in (0, 1):
         @pl.when(core == me)
         def _():
@@ -324,8 +329,6 @@
                         if_known(relay(slot, p), lambda copy: copy.wait_send())
                 for slot in CROSSED[me]:
                     if_known(cross(slot, p), lambda copy: copy.wait_send())
-    for copy in stores:
-        copy.wait()
 
 
 def body(count, queries, keys, values, lengths):
@@ -335,27 +338,25 @@
     group = heads // kv_heads
     return pl.pallas_call(
         functools.partial(kernel, count),
-        out_shape=jax.ShapeDtypeStruct((toks, wide), jnp.bfloat16),
-        in_specs=[pl.BlockSpec(memory_space=pl.ANY)] * 3 + [pl.BlockSpec(memory_space=pltpu.SMEM)],
-        out_specs=pl.BlockSpec(memory_space=pl.ANY),
+        out_shape=pltpu.VMEM((toks, wide), jnp.bfloat16),
+        in_specs=[pl.BlockSpec(memory_space=pltpu.HBM)] * 3 + [pl.BlockSpec(memory_space=pltpu.SMEM)],
+        out_specs=pl.BlockSpec(memory_space=pltpu.VMEM),
         scratch_shapes=[
             pltpu.VMEM((SLOTS, 2, kv_heads, toks, HEAD_DIM), jnp.bfloat16),
             pltpu.VMEM((toks, wide), jnp.bfloat16),
-            pltpu.VMEM((kv_heads, group, HEAD_DIM, toks), jnp.bfloat16),
-            pltpu.VMEM((kv_heads, group, HEAD_DIM, toks), jnp.float32),
-            pltpu.VMEM((kv_heads, group, toks), jnp.float32),
-            pltpu.VMEM((kv_heads, group, toks), jnp.float32),
+            pltpu.VMEM((kv_heads, group // PAIR, HEAD_DIM, PAIR * toks), jnp.bfloat16),
+            pltpu.VMEM((kv_heads, group // PAIR, HEAD_DIM, PAIR * toks), jnp.float32),
+            pltpu.VMEM((kv_heads, group // PAIR, 1, PAIR * toks), jnp.float32),
+            pltpu.VMEM((kv_heads, group // PAIR, 1, PAIR * toks), jnp.float32),
             pltpu.VMEM((2, HEAD_DIM), jnp.float32),
             pltpu.VMEM((2, toks, HEAD_DIM), jnp.bfloat16),
-            pltpu.VMEM((HEAD_DIM, toks), jnp.bfloat16),
-            pltpu.VMEM((2, PAIR, toks, toks), jnp.float32),
-            pltpu.VMEM((2, PAIR, toks, toks), jnp.bfloat16),
-            pltpu.VMEM((2, PAIR, toks), jnp.float32),
-            pltpu.VMEM((2, PAIR, toks), jnp.float32),
-            pltpu.VMEM((2, PAIR, toks), jnp.float32),
-            pltpu.VMEM((toks, wide), jnp.bfloat16),
+            pltpu.VMEM((HEAD_DIM, PAIR * toks), jnp.bfloat16),
+            pltpu.VMEM((2, toks, PAIR * toks), jnp.float32),
+            pltpu.VMEM((2, toks, PAIR * toks), jnp.bfloat16),
+            pltpu.VMEM((2, 1, PAIR * toks), jnp.float32),
+            pltpu.VMEM((2, 1, PAIR * toks), jnp.float32),
+            pltpu.VMEM((2, 1, PAIR * toks), jnp.float32),
             pltpu.SemaphoreType.DMA((5,)),
-            pltpu.SemaphoreType.DMA((2,)),
             pltpu.SemaphoreType.DMA((SLOTS, 4)),
             pltpu.SemaphoreType.DMA((4, 4)),
             pltpu.SemaphoreType.DMA((SLOTS, 4)),

time: 42.6 us -> 42.2 us (level)
  local copies, waits for them, and re-layouts: 2.06 us -> 0.88 us
  Pallas kernels: 40.3 us -> 41.2 us
    unnamed x1, local copies, waits for them, and re-layouts: 2.06 us -> 0.88 us
    pallas_call x1, Pallas kernels: 40.3 us -> 41.2 us  [body(): pl.pallas_call(functools.partial(kernel, count), out_shape=pltpu.VMEM((to...]
where the time goes in v4:
time: 42.2 us; the launch traced here: 42.1 us
  Pallas kernels  41.2 us (98%)
  local copies, waits for them, and re-layouts  0.88 us (2%)
    pallas_call x1, Pallas kernels, body(): pl.pallas_call(functools.partial(kernel, count), out_shape=pltpu.VMEM((to...  41.2 us
    unnamed x1, local copies, waits for them, and re-layouts  0.88 us

profile of v4, /device:TPU:249, one launch (start us, length us, event | category | flops | bytes accessed | tf_op | source)
XLA Modules:
  0.0 42.1 jit_solution(9693494895116783428)
XLA Ops:
  0.0 41.2 %shard_map.46 = bf16[384,1024]{1,0:T(8,128)(2,1)S(1)} custom-call(bf16[384,1024]{1,0:T(8,128)(2,1)} %q_hbm.1, bf16[384,256]{1,0:T(8,128)(2,1)} %k_hbm.1, bf16[384,256]{1,0:T(8,128)(2,1)} %v_hbm.1, s32[32]{0:T(128)} %lengths.1), custom_call_target="tpu_custom_call" | custom-call | tf_op jit(solution)/shard_map/pallas_call | solution.py:339
  41.2 0.9 %copy.6 = bf16[384,1024]{1,0:T(8,128)(2,1)} copy(bf16[384,1024]{1,0:T(8,128)(2,1)S(1)} %shard_map.46) | data formatting | bytes 1572864

commit v5 on v4

--- a/solution.py
+++ b/solution.py
@@ -31,8 +31,9 @@
      2: ((1, FIRST), (RELAY, (0,)), (SPARE, (0,)), (0, FIRST)),
      4: ((RELAY, (1,)), (SPARE, (1,)), (1, SECOND), (0, SECOND)),
      6: ((RELAY, (2,)), (SPARE, (2, 3)), (3, FIRST), (2, FIRST)),
-     8: ((RELAY, (3,)), (LANDED, (0, 1)), (3, (2,)), (LANDED, (2,)), (3, (3,)), (LANDED, (3,)), (2, SECOND)),
-     10: ((5, (0,)), (5, (2,)), (5, (1,))), 11: ((5, (3,)), (4, FIRST)), 13: ((4, SECOND),)},
+     7: ((RELAY, (3,)), (LANDED, (0,))),
+     8: ((LANDED, (1,)), (3, SECOND), (2, SECOND)), 9: ((LANDED, (2,)),),
+     10: ((LANDED, (3,)), (5, (0,)), (5, (2,)), (5, (1,))), 11: ((5, (3,)), (4, FIRST)), 13: ((4, SECOND),)},
 )
 OWN_LANES = ((0, 1), (0, 2, 3))
 RELAYED = ((0, 2), (1, 3, RELAY, LANDED, SPARE))
@@ -215,14 +216,14 @@
     scores[1] = jnp.full(scores.shape[1:], MASKED, jnp.float32)
     weights[...] = jnp.zeros_like(weights)
 
-    mark(1, cp)
+    mark(OWN, cp)
 
     def own_body(head, carry):
         keys = kv[OWN, 0, head]
         values = kv[OWN, 1, head].T
         causal = lax.broadcasted_iota(jnp.int32, (toks, toks), 0) <= lax.broadcasted_iota(jnp.int32, (toks, toks), 1)
         for half in range(group // PAIR):
-            found = product(keys, 1, head, half)
+            found = product(keys, OWN, head, half)
             found = jnp.concatenate(
                 [jnp.where(causal, found[:, k * toks : (k + 1) * toks], MASKED) for k in range(PAIR)], axis=1)
             new = jnp.max(found, axis=0, keepdims=True)
@@ -234,6 +235,13 @@
 
     lax.fori_loop(0, kv_heads, own_body, 0)
 
+    def mark_body(slot, carry):
+        far_block = jnp.where(core == 0, 2 * chip - 7, 2 * chip)
+        mark(slot, jnp.where(slot == FAR, far_block, 2 * (chip - slot // 2 - 1) + lax.rem(slot, 2)))
+        return carry
+
+    lax.fori_loop(0, FAR + 1, mark_body, 0)
+
     def where_is(step):
         in_pairs = jnp.where(core == 0, jnp.where(step < 8, step, step - 2), step - 2)
         far = jnp.where(core == 0, (step == 8) | (step == 9), step < 2)
@@ -242,12 +250,10 @@
         parity = lax.rem(in_pairs + step // 10, 2)
         slot = jnp.where(far, FAR, 2 * distance + parity)
         head = jnp.where(far, lax.rem(step, 2), lax.rem(in_pairs, 4) // 2)
-        far_block = jnp.where(core == 0, 2 * chip - 7, 2 * chip)
-        block = jnp.where(far, far_block, 2 * (chip - distance - 1) + parity)
-        return slot, head, block
+        return slot, head
 
     def score(slot, head, half):
-        keys, side = kv[slot, 0, head], lax.rem(slot, 2)
+        keys, side = kv[slot, 0, head], slot
         for cut in cuts:
             found = product(keys, side, head, half, cut)
             scores[half, :, cut] = found
@@ -279,14 +285,10 @@
             out[:, first : first + HEAD_DIM] = (acc[head, half, :, cut] * share).astype(out.dtype).T
 
     def step_body(step, carry):
-        @pl.when(step == STEPS - 1)
-        def _():
-            finish(0)
-
         for quarter in range((STEPS + 3) // 4):
             @pl.when(step // 4 == quarter)
             def _():
-                for s in range(4 * quarter, 4 * quarter + 4):
+                for s in range(4 * quarter, min(4 * quarter + 4, STEPS - 1)):
                     for me in (0, 1):
                         if s in AHEAD[me]:
                             @pl.when((step == s) & (core == me))
@@ -294,12 +296,8 @@
                                 for slot, pieces in AHEAD[me][s]:
                                     event(me, slot, pieces)
 
-        slot, head, block = where_is(step)
-        last_slot, last_head, _ = where_is(jnp.maximum(step - 1, 0))
-
-        @pl.when(head == 0)
-        def _():
-            mark(lax.rem(slot, 2), block)
+        slot, head = where_is(step)
+        last_slot, last_head = where_is(jnp.maximum(step - 1, 0))
 
         values = kv[last_slot, 1, last_head].T
         weigh(last_head, 1)
@@ -310,14 +308,28 @@
         weigh(head, 0)
         return carry
 
-    lax.fori_loop(0, STEPS, step_body, 0)
-    last_slot, last_head, _ = where_is(jnp.int32(STEPS - 1))
+    lax.fori_loop(0, STEPS - 1, step_body, 0)
+    last_slot, last_head = where_is(jnp.int32(STEPS - 2))
     values = kv[last_slot, 1, last_head].T
     weigh(last_head, 1)
     gather(last_head, 0, values)
     gather(last_head, 1, values)
-
-    finish(kv_heads - 1)
+    for head in range(kv_heads - 1):
+        finish(head)
+    for me in (0, 1):
+        @pl.when(core == me)
+        def _():
+            for slot, pieces in AHEAD[me][STEPS - 1]:
+                event(me, slot, pieces)
+
+    head = kv_heads - 1
+    values = kv[4, 1, head].T
+    score(4, head, 0)
+    score(4, head, 1)
+    for half in range(group // PAIR):
+        weigh(head, half)
+        gather(head, half, values)
+    finish(head)
     for me in (0, 1):
         @pl.when(core == me)
         def _():
@@ -349,7 +361,7 @@
             pltpu.VMEM((kv_heads, group // PAIR, 1, PAIR * toks), jnp.float32),
             pltpu.VMEM((kv_heads, group // PAIR, 1, PAIR * toks), jnp.float32),
             pltpu.VMEM((2, HEAD_DIM), jnp.float32),
-            pltpu.VMEM((2, toks, HEAD_DIM), jnp.bfloat16),
+            pltpu.VMEM((SLOTS, toks, HEAD_DIM), jnp.bfloat16),
             pltpu.VMEM((HEAD_DIM, PAIR * toks), jnp.bfloat16),
             pltpu.VMEM((2, toks, PAIR * toks), jnp.float32),
             pltpu.VMEM((2, toks, PAIR * toks), jnp.bfloat16),

time: 42.2 us -> 40.8 us (0.967)
  the two profiles are of different devices: /device:TPU:249 before, /device:TPU:253 now
where the time goes in v5:
time: 40.8 us; the launch traced here: 40.7 us
  Pallas kernels  39.8 us (98%)
  local copies, waits for them, and re-layouts  0.88 us (2%)
    pallas_call x1, Pallas kernels, body(): pl.pallas_call(functools.partial(kernel, count), out_shape=pltpu.VMEM((to...  39.8 us
    unnamed x1, local copies, waits for them, and re-layouts  0.88 us

profile of v5, /device:TPU:253, one launch (start us, length us, event | category | flops | bytes accessed | tf_op | source)
XLA Modules:
  0.0 40.7 jit_solution(14293370371397764654)
XLA Ops:
  0.0 39.8 %shard_map.46 = bf16[384,1024]{1,0:T(8,128)(2,1)S(1)} custom-call(bf16[384,1024]{1,0:T(8,128)(2,1)} %q_hbm.1, bf16[384,256]{1,0:T(8,128)(2,1)} %k_hbm.1, bf16[384,256]{1,0:T(8,128)(2,1)} %v_hbm.1, s32[32]{0:T(128)} %lengths.1), custom_call_target="tpu_custom_call" | custom-call | tf_op jit(solution)/shard_map/pallas_call | solution.py:351
  39.8 0.9 %copy.6 = bf16[384,1024]{1,0:T(8,128)(2,1)} copy(bf16[384,1024]{1,0:T(8,128)(2,1)S(1)} %shard_map.46) | data formatting | bytes 1572864

commit v6 on v5

--- a/solution.py
+++ b/solution.py
@@ -17,26 +17,25 @@
 LANDED = 7
 RELAY = 8
 OWN = 9
-SPARE = 10
-SLOTS = 11
+SLOTS = 10
 FIRST, SECOND = (0, 1), (2, 3)
 STEPS = 14
-SHORT_WAY = (2, 3)
+SHORT_WAY = (3,)
 AHEAD = (
     {0: ((0, FIRST),), 1: ((1, FIRST),), 2: ((0, SECOND),), 3: ((1, SECOND),),
      4: ((2, FIRST),), 5: ((3, FIRST),), 6: ((2, SECOND),), 7: ((3, SECOND),),
      8: ((FAR, FIRST),), 9: ((FAR, SECOND),),
      10: ((4, (0,)), (5, FIRST)), 11: ((4, (1,)),), 12: ((5, SECOND), (4, (2,))), 13: ((4, (3,)),)},
     {0: ((FAR, FIRST),), 1: ((FAR, SECOND),),
-     2: ((1, FIRST), (RELAY, (0,)), (SPARE, (0,)), (0, FIRST)),
-     4: ((RELAY, (1,)), (SPARE, (1,)), (1, SECOND), (0, SECOND)),
-     6: ((RELAY, (2,)), (SPARE, (2, 3)), (3, FIRST), (2, FIRST)),
+     2: ((1, FIRST), (RELAY, (0,)), (0, FIRST)),
+     4: ((RELAY, (1,)), (1, SECOND), (0, SECOND)),
+     6: ((RELAY, (2,)), (3, FIRST), (2, FIRST)),
      7: ((RELAY, (3,)), (LANDED, (0,))),
      8: ((LANDED, (1,)), (3, SECOND), (2, SECOND)), 9: ((LANDED, (2,)),),
-     10: ((LANDED, (3,)), (5, (0,)), (5, (2,)), (5, (1,))), 11: ((5, (3,)), (4, FIRST)), 13: ((4, SECOND),)},
+     10: ((LANDED, (3,)), (5, (0, 1))), 11: ((5, SECOND), (4, FIRST)), 13: ((4, SECOND),)},
 )
-OWN_LANES = ((0, 1), (0, 2, 3))
-RELAYED = ((0, 2), (1, 3, RELAY, LANDED, SPARE))
+OWN_LANES = ((0, 1), (2, 0))
+RELAYED = ((0, 2), (1, 3, RELAY, LANDED))
 CROSSED = ((0, 2, 4), (1, 3, LANDED, 5))
 
 
@@ -67,15 +66,10 @@
     relay_to, relay_owner = core_of(reader), core_of(jnp.maximum(reader - 4, 0))
     relay_from = core_of(row + lax.rem(y + 1, RING_Y))
     has_landed = chip >= 4
-    owner_chip, reader_chip = chips - 4, chips - 1
-    between_chip = owner_chip - owner_chip % RING_Y + (owner_chip + RING_Y - 3) % RING_Y
-    is_owner, is_between, is_reader = chip == owner_chip, chip == between_chip, chip == reader_chip
 
     def holds(slot, me):
         if slot == RELAY:
             return has_relay
-        if slot == SPARE:
-            return is_between
         if slot == LANDED or (slot == FAR and me == 0):
             return has_landed
         if slot == FAR or slot == OWN:
@@ -115,28 +109,30 @@
 
     @pl.when(core == 1)
     def _():
-        greet(near + ((goes_down, down), (has_relay, relay_owner), (has_relay, relay_to), (has_landed, relay_from),
-                      (is_owner | is_reader, core_of(between_chip)),
-                      (is_between, core_of(owner_chip)), (is_between, core_of(reader_chip))))
+        greet(near + ((goes_down, down), (has_relay, relay_owner), (has_relay, relay_to), (has_landed, relay_from)))
 
     for copy in loads[:4]:
         copy.wait()
 
     def own_send(lane, p):
-        to, slot = ((after, core), (partner, FAR), (down, RELAY), (core_of(between_chip), SPARE))[lane]
-        return (has_after, chip >= 0, goes_down, is_owner)[lane], remote(
+        to, slot = ((after, core), (partner, FAR), (down, RELAY))[lane]
+        return (has_after, chip >= 0, goes_down)[lane], remote(
             piece(OWN, p), piece(slot, p), own_sem.at[lane, p], recv_sem.at[slot, p], to)
 
     def relay(slot, p):
         to, target = {0: (after, 2), 1: (after, 3), 2: (after, 4), 3: (after, 5),
-                      RELAY: (relay_to, LANDED), LANDED: (before, 5), SPARE: (core_of(reader_chip), 5)}[slot]
+                      RELAY: (relay_to, LANDED), LANDED: (before, 5)}[slot]
         known = holds(slot, 1)
         if slot < FAR:
             known = known & has_after
+        if slot == 3 and p not in SHORT_WAY:
+            known = known & (y == RING_Y - 2)
+        if slot == LANDED:
+            known = known & (y != 0)
         return known, remote(piece(slot, p), piece(target, p), relay_sem.at[slot, p], recv_sem.at[target, p], to)
 
     def relayed(me, slot, p):
-        if slot == 3 and p not in SHORT_WAY or slot in (LANDED, SPARE) and p in SHORT_WAY:
+        if slot == LANDED and p in SHORT_WAY:
             return False
         return slot in RELAYED[me]
 
@@ -370,7 +366,7 @@
             pltpu.VMEM((2, 1, PAIR * toks), jnp.float32),
             pltpu.SemaphoreType.DMA((5,)),
             pltpu.SemaphoreType.DMA((SLOTS, 4)),
-            pltpu.SemaphoreType.DMA((4, 4)),
+            pltpu.SemaphoreType.DMA((3, 4)),
             pltpu.SemaphoreType.DMA((SLOTS, 4)),
             pltpu.SemaphoreType.DMA((SLOTS, 4)),
         ],

time: 40.8 us -> 40.7 us (level)
  the two profiles are of different devices: /device:TPU:253 before, /device:TPU:257 now
where the time goes in v6:
time: 40.7 us; the launch traced here: 40.6 us
  Pallas kernels  39.7 us (98%)
  local copies, waits for them, and re-layouts  0.88 us (2%)
    pallas_call x1, Pallas kernels, body(): pl.pallas_call(functools.partial(kernel, count), out_shape=pltpu.VMEM((to...  39.7 us
    unnamed x1, local copies, waits for them, and re-layouts  0.88 us

profile of v6, /device:TPU:257, one launch (start us, length us, event | category | flops | bytes accessed | tf_op | source)
XLA Modules:
  0.0 40.6 jit_solution(10260301426520854836)
XLA Ops:
  0.0 39.7 %shard_map.46 = bf16[384,1024]{1,0:T(8,128)(2,1)S(1)} custom-call(bf16[384,1024]{1,0:T(8,128)(2,1)} %q_hbm.1, bf16[384,256]{1,0:T(8,128)(2,1)} %k_hbm.1, bf16[384,256]{1,0:T(8,128)(2,1)} %v_hbm.1, s32[32]{0:T(128)} %lengths.1), custom_call_target="tpu_custom_call" | custom-call | tf_op jit(solution)/shard_map/pallas_call | solution.py:347
  39.7 0.9 %copy.6 = bf16[384,1024]{1,0:T(8,128)(2,1)} copy(bf16[384,1024]{1,0:T(8,128)(2,1)S(1)} %shard_map.46) | data formatting | bytes 1572864
